TPU v7x, 256 devices: a whole 4x4x8 slice. The times are simulated.
256 devices in a mesh: gz: 16 (over y_lo, z), ang: 16 (over x, y_hi, core).
Axes of the slice: x: 4, y: 4 (y_hi: 2, y_lo: 2; y = y_hi * 2 + y_lo), z: 8, core: 2. Of those that a mesh axis runs over, the one named last changes fastest.
Arguments:
- fan_views: bfloat16 [16, 64, 128, 896], P('gz', None, 'ang'), may hold values from -6 to 6
- rebin_weight: bfloat16 [896, 896], replicated, may hold values from -0.1875 to 0.1875
- slab_table: int32 [16, 16, 1], P('gz'), may hold values from 0 to 15; in each aligned block of 16 rows (0 to 15, 16 to 31, ..., all dimensions but the last counted through in order) at most 2 rows name the same one
- slice_offset: int32 [16, 16], P('gz'), may hold values from 0 to 60
- tiles: bfloat16 [2048, 896, 128], P('ang'), may hold values from -0.015625 to 0.015625
- tile_view: int32 [2048], P('ang'), may hold values from 0 to 7, as said below
Outputs:
- volume: float32 [512, 2048], P(('gz', 'ang'))
Inputs may be any that keep to these rules, and one draw needn't show every extreme that they name: `slab_table`: entry [t, b, 0] is the slab receiving row block b of turn t; one turn sends at most 2 row blocks to one slab. `tile_view`: the 8 entries of each aligned run (one angle group and one pixel block) are a permutation of 0 to 7.
All inputs are finite; a program needn't handle non-finite values.
Results may differ from a plain program's by a relative error of at most 0.0059.
Values may be sent and summed in bfloat16 or wider, within the bound.
A program may use at most 128 MiB of HBM per device.

v0:
```python
import math

import jax
import jax.numpy as jnp
from jax import lax
from jax.sharding import PartitionSpec as P

COLS = 896
BR = 4
CAP = 2
HALO = 16
TILE_PIX = 128
ZD = 32
BLOCKS = 16
PIXBLK = 16
ZE = 64


def from_behind(shard, axis, by):
    devices = lax.axis_size(axis)
    pairs = [(i, i + by) for i in range(devices) if 0 <= i + by < devices]
    return lax.ppermute(shard, axis, pairs)


def in_blocks(shard, dim, devices):
    before, after = (shard.shape[:dim], shard.shape[dim + 1 :])
    return jnp.moveaxis(shard.reshape(*before, devices, -1, *after), dim, 0)


def summed_on_arrival(shard, axis, dim):
    devices = lax.axis_size(axis)
    blocks = lax.all_to_all(in_blocks(shard, dim, devices), axis, 0, 0, tiled=True)
    return jnp.sum(blocks, axis=0)


def filter_tables(columns):
    column_index = jnp.arange(columns, dtype=jnp.int32)
    phase_steps = column_index[:, None] * column_index[None, :] % columns
    radians = phase_steps.astype(jnp.float32) * (2.0 * math.pi / columns)
    dft_table = jnp.concatenate([jnp.cos(radians), jnp.sin(radians)], axis=1).astype(jnp.bfloat16)
    frequency = jnp.minimum(column_index, columns - column_index).astype(jnp.float32) * (
        2.0 / (columns * columns)
    )
    ramp_weight = jnp.concatenate([frequency, frequency])
    return (dft_table, ramp_weight)


def ramp_filter(values, dft_table, ramp_weight):
    spectrum = jnp.dot(values, dft_table, preferred_element_type=jnp.float32)
    weighted = (spectrum * ramp_weight).astype(jnp.bfloat16)
    result = lax.dot_general(
        weighted, dft_table, (((1,), (1,)), ((), ())), preferred_element_type=jnp.float32
    )
    return result.astype(jnp.bfloat16)


def backproject(filtered, weights, view_order):
    pieces = []
    for pixel_block in range(weights.shape[0]):
        chosen = jnp.take(filtered, view_order[pixel_block], axis=1).reshape(filtered.shape[0], -1)
        pieces.append(jnp.dot(chosen, weights[pixel_block], preferred_element_type=jnp.float32))
    return jnp.concatenate(pieces, axis=1)


def row_route(
    parallel, dft_table, ramp_weight, weights, view_order, destination, offsets, views_dev
):
    slab_count = lax.axis_size("gz")
    slot_count = slab_count * CAP
    blocks_flat = parallel.reshape(BLOCKS, BR * views_dev * COLS)
    block_index = jnp.arange(BLOCKS, dtype=jnp.int32)
    earlier = block_index[None, :] < block_index[:, None]
    same_slab = destination[:, None] == destination[None, :]
    slot_rank = jnp.sum(same_slab & earlier, axis=1)
    slot_index = destination * CAP + slot_rank
    chosen = slot_index[None, :] == jnp.arange(slot_count, dtype=jnp.int32)[:, None]
    packed = jnp.dot(
        chosen.astype(jnp.bfloat16), blocks_flat, preferred_element_type=jnp.float32
    ).astype(jnp.bfloat16)
    packed = packed.reshape(slab_count, CAP, BR * views_dev, COLS)
    slot_offset = jnp.sum(jnp.where(chosen, offsets[None, :] + 1, 0), axis=1) - 1
    slot_offset = slot_offset.reshape(slab_count, CAP)
    payload = lax.all_to_all(packed, "gz", split_axis=0, concat_axis=0, tiled=True)
    settle_slot_offset = lax.all_to_all(slot_offset, "gz", split_axis=0, concat_axis=0, tiled=True)
    filtered = ramp_filter(payload.reshape(-1, COLS), dft_table, ramp_weight)
    payload, arrived = (filtered.reshape(payload.shape), settle_slot_offset)
    received = payload.reshape(slot_count * BR, views_dev, COLS)
    back = backproject(received, weights, view_order)
    first_slice = arrived.reshape(-1, 1)
    row_slice = (first_slice + jnp.arange(BR, dtype=jnp.int32)[None, :]).reshape(-1)
    row_slice = jnp.where(jnp.repeat(first_slice.reshape(-1), BR) >= 0, row_slice, -1)
    placement = (row_slice[None, :] == jnp.arange(ZE, dtype=jnp.int32)[:, None]).astype(jnp.float32)
    extended = jnp.dot(
        placement, back, precision=lax.Precision.HIGHEST, preferred_element_type=jnp.float32
    )
    from_below = from_behind(extended[ZE - HALO :].astype(jnp.bfloat16), "gz", 1).astype(
        jnp.float32
    )
    from_above = from_behind(extended[:HALO].astype(jnp.bfloat16), "gz", -1).astype(jnp.float32)
    interior = extended[HALO : HALO + ZD]
    interior = (
        interior
        + jnp.pad(from_below, ((0, ZD - HALO), (0, 0)))
        + jnp.pad(from_above, ((ZD - HALO, 0), (0, 0)))
    )
    return summed_on_arrival(interior, "ang", 0)


def on_device(fan_views, rebin_weight, slab_table, slice_offset, tiles, tile_view):
    dft_table, ramp_weight = filter_tables(COLS)
    views_dev = fan_views.shape[2]
    parallel = jnp.dot(
        fan_views.reshape(-1, COLS), rebin_weight, preferred_element_type=jnp.float32
    ).astype(jnp.bfloat16)
    weights = tiles.reshape(PIXBLK, views_dev * COLS, TILE_PIX)
    view_order = tile_view.reshape(PIXBLK, views_dev)
    destination = slab_table[0, :, 0]
    offsets = slice_offset[0]
    result = row_route(
        parallel, dft_table, ramp_weight, weights, view_order, destination, offsets, views_dev
    )
    return result


def solution(mesh):
    in_specs = (
        P("gz", None, "ang", None),
        P(),
        P("gz", None, None),
        P("gz", None),
        P("ang", None, None),
        P("ang"),
    )
    out_specs = P(("gz", "ang"), None)
    return jax.shard_map(
        on_device, mesh=mesh, in_specs=in_specs, out_specs=out_specs, check_vma=False
    )
```

profile of v0, /device:TPU:1, one launch (start us, length us, event | category | flops | bytes accessed | tf_op | source)
XLA Modules:
  0.0 184.2 jit_solution(200598162686159785)
XLA Ops:
  0.0 1.0 convert_reduce_fusion
  3.1 10.1 %all-to-all-start = ((s32[16,1,2]{2,1,0:T(1,128)}), s32[16,1,2]{2,1,0:T(1,128)S(1)}, u32[]{:S(2)}, u32[]{:S(2)}) async-start(s32[16,1,2]{2,1,0:T(1,128)} %bitcast.2), calls=%async_computation | async-start | bytes 16384 | tf_op jit(solution)/shard_map/all_to_all | solution.py:84
  13.2 3.3 %convolution_convert_fusion.1 = bf16[512,896]{1,0:T(8,128)(2,1)} fusion(bf16[896,896]{1,0:T(8,128)(2,1)S(1)} %copy-done, bf16[1,64,8,896]{3,2,1,0:T(8,128)(2,1)} %param.8), kind=kOutput, calls=%fused_computation.110 | convolution fusion | flops 822542336 | bytes 3440640 | tf_op jit(solution)/shard_map/dot_general | solution.py:112
  16.5 1.6 reshape.158
  18.9 1.5 copy.105
  20.5 7.6 %all-to-all-start.1 = ((bf16[16,2,32,896]{3,2,1,0:T(8,128)(2,1)}), bf16[16,2,32,896]{3,2,1,0:T(8,128)(2,1)S(1)}, u32[]{:S(2)}, u32[]{:S(2)}) async-start(bf16[16,2,32,896]{3,2,1,0:T(8,128)(2,1)} %bitcast.40), calls=%async_computation.1 | async-start | bytes 3670016 | tf_op jit(solution)/shard_map/all_to_all | solution.py:83
  28.1 0.7 compare_and_fusion
  29.0 14.5 %sine_convert_fusion = (bf16[896,896]{1,0:T(8,128)(2,1)S(1)}, bf16[896,896]{1,0:T(8,128)(2,1)}) fusion(), kind=kLoop, calls=%fused_computation.22 | loop fusion | flops 8830976 | bytes 3211264 | tf_op jit(solution)/shard_map/convert.7
  45.1 24.6 %all-to-all-done.1 = bf16[16,2,32,896]{3,2,1,0:T(8,128)(2,1)S(1)} async-done(((bf16[16,2,32,896]{3,2,1,0:T(8,128)(2,1)}), bf16[16,2,32,896]{3,2,1,0:T(8,128)(2,1)S(1)}, u32[]{:S(2)}, u32[]{:S(2)}) %all-to-all-start.1) | async-done | bytes 1835040 | tf_op jit(solution)/shard_map/all_to_all | solution.py:83
  69.7 10.9 %convert_bitcast_fusion = bf16[128,8,896]{2,1,0:T(8,128)(2,1)} fusion(bf16[896,896]{1,0:T(8,128)(2,1)S(1)} %get-tuple-element.72, bf16[896,896]{1,0:T(8,128)(2,1)} %get-tuple-element.73, bf16[1024,896]{1,0:T(8,128)(2,1)S(1)} %bitcast.195, f32[1792]{0:T(1024)S(1)} %pad_maximum_fusion.7), kind=kOutput, calls=%fused_computation.93 | convolution fusion | flops 6594101248 | bytes 6888448 | tf_op jit(solution)/shard_map/dot_general | solution.py:51
  80.6 1.8 copy.57
  82.4 2.0 %gather_fusion = bf16[8,128,896]{2,1,0:T(8,128)(2,1)} fusion(bf16[128,8,896]{2,0,1:T(8,128)(2,1)S(1)} %copy.57, s32[1024]{0:T(1024)S(1)} %get-tuple-element.89), kind=kCustom, calls=%fused_computation.clone | custom fusion | bytes 3670048 | tf_op jit(solution)/shard_map/jit(_take)/gather | solution.py:60
  84.4 2.0 %gather_fusion.1 = bf16[8,128,896]{2,1,0:T(8,128)(2,1)} fusion(bf16[128,8,896]{2,0,1:T(8,128)(2,1)S(1)} %copy.57, s32[1024]{0:T(1024)S(1)} %get-tuple-element.88), kind=kCustom, calls=%fused_computation.1.clone | custom fusion | bytes 3670048 | tf_op jit(solution)/shard_map/jit(_take)/gather | solution.py:60
  86.4 2.1 %gather_fusion.2 = bf16[8,128,896]{2,1,0:T(8,128)(2,1)} fusion(bf16[128,8,896]{2,0,1:T(8,128)(2,1)S(1)} %copy.57, s32[1024]{0:T(1024)S(1)} %get-tuple-element.87), kind=kCustom, calls=%fused_computation.2.clone | custom fusion | bytes 3670048 | tf_op jit(solution)/shard_map/jit(_take)/gather | solution.py:60
  88.5 2.0 %gather_fusion.3 = bf16[8,128,896]{2,1,0:T(8,128)(2,1)} fusion(bf16[128,8,896]{2,0,1:T(8,128)(2,1)S(1)} %copy.57, s32[1024]{0:T(1024)S(1)} %get-tuple-element.86), kind=kCustom, calls=%fused_computation.3.clone | custom fusion | bytes 3670048 | tf_op jit(solution)/shard_map/jit(_take)/gather | solution.py:60
  90.5 2.0 %gather_fusion.4 = bf16[8,128,896]{2,1,0:T(8,128)(2,1)} fusion(bf16[128,8,896]{2,0,1:T(8,128)(2,1)S(1)} %copy.57, s32[1024]{0:T(1024)S(1)} %get-tuple-element.85), kind=kCustom, calls=%fused_computation.4.clone | custom fusion | bytes 3670048 | tf_op jit(solution)/shard_map/jit(_take)/gather | solution.py:60
  92.5 2.0 %gather_fusion.5 = bf16[8,128,896]{2,1,0:T(8,128)(2,1)} fusion(bf16[128,8,896]{2,0,1:T(8,128)(2,1)S(1)} %copy.57, s32[1024]{0:T(1024)S(1)} %get-tuple-element.84), kind=kCustom, calls=%fused_computation.5.clone | custom fusion | bytes 3670048 | tf_op jit(solution)/shard_map/jit(_take)/gather | solution.py:60
  94.5 2.0 %gather_fusion.6 = bf16[8,128,896]{2,1,0:T(8,128)(2,1)} fusion(bf16[128,8,896]{2,0,1:T(8,128)(2,1)S(1)} %copy.57, s32[1024]{0:T(1024)S(1)} %get-tuple-element.83), kind=kCustom, calls=%fused_computation.6.clone | custom fusion | bytes 3670048 | tf_op jit(solution)/shard_map/jit(_take)/gather | solution.py:60
  96.5 2.0 %gather_fusion.7 = bf16[8,128,896]{2,1,0:T(8,128)(2,1)} fusion(bf16[128,8,896]{2,0,1:T(8,128)(2,1)S(1)} %copy.57, s32[1024]{0:T(1024)S(1)} %get-tuple-element.82), kind=kCustom, calls=%fused_computation.7.clone | custom fusion | bytes 3670048 | tf_op jit(solution)/shard_map/jit(_take)/gather | solution.py:60
  98.5 2.0 %gather_fusion.8 = bf16[8,128,896]{2,1,0:T(8,128)(2,1)} fusion(bf16[128,8,896]{2,0,1:T(8,128)(2,1)S(1)} %copy.57, s32[1024]{0:T(1024)S(1)} %get-tuple-element.81), kind=kCustom, calls=%fused_computation.8.clone | custom fusion | bytes 3670048 | tf_op jit(solution)/shard_map/jit(_take)/gather | solution.py:60
  100.5 2.1 %gather_fusion.9 = bf16[8,128,896]{2,1,0:T(8,128)(2,1)} fusion(bf16[128,8,896]{2,0,1:T(8,128)(2,1)S(1)} %copy.57, s32[1024]{0:T(1024)S(1)} %get-tuple-element.80), kind=kCustom, calls=%fused_computation.9.clone | custom fusion | bytes 3670048 | tf_op jit(solution)/shard_map/jit(_take)/gather | solution.py:60
  102.6 2.0 %gather_fusion.10 = bf16[8,128,896]{2,1,0:T(8,128)(2,1)} fusion(bf16[128,8,896]{2,0,1:T(8,128)(2,1)S(1)} %copy.57, s32[1024]{0:T(1024)S(1)} %get-tuple-element.79), kind=kCustom, calls=%fused_computation.10.clone | custom fusion | bytes 3670048 | tf_op jit(solution)/shard_map/jit(_take)/gather | solution.py:60
  104.6 2.0 %gather_fusion.11 = bf16[8,128,896]{2,1,0:T(8,128)(2,1)} fusion(bf16[128,8,896]{2,0,1:T(8,128)(2,1)S(1)} %copy.57, s32[1024]{0:T(1024)S(1)} %get-tuple-element.78), kind=kCustom, calls=%fused_computation.11.clone | custom fusion | bytes 3670048 | tf_op jit(solution)/shard_map/jit(_take)/gather | solution.py:60
  106.5 2.0 %gather_fusion.12 = bf16[8,128,896]{2,1,0:T(8,128)(2,1)} fusion(bf16[128,8,896]{2,0,1:T(8,128)(2,1)S(1)} %copy.57, s32[1024]{0:T(1024)S(1)} %get-tuple-element.77), kind=kCustom, calls=%fused_computation.12.clone | custom fusion | bytes 3670048 | tf_op jit(solution)/shard_map/jit(_take)/gather | solution.py:60
  108.6 2.0 %gather_fusion.13 = bf16[8,128,896]{2,1,0:T(8,128)(2,1)} fusion(bf16[128,8,896]{2,0,1:T(8,128)(2,1)S(1)} %copy.57, s32[1024]{0:T(1024)S(1)} %get-tuple-element.76), kind=kCustom, calls=%fused_computation.13.clone | custom fusion | bytes 3670048 | tf_op jit(solution)/shard_map/jit(_take)/gather | solution.py:60
  110.6 2.1 %gather_fusion.14 = bf16[8,128,896]{2,1,0:T(8,128)(2,1)} fusion(bf16[128,8,896]{2,0,1:T(8,128)(2,1)S(1)} %copy.57, s32[1024]{0:T(1024)S(1)} %get-tuple-element.75), kind=kCustom, calls=%fused_computation.14.clone | custom fusion | bytes 3670048 | tf_op jit(solution)/shard_map/jit(_take)/gather | solution.py:60
  112.7 2.0 %gather_fusion.15 = bf16[8,128,896]{2,1,0:T(8,128)(2,1)} fusion(bf16[128,8,896]{2,0,1:T(8,128)(2,1)S(1)} %copy.57, s32[1024]{0:T(1024)S(1)} %get-tuple-element.74), kind=kCustom, calls=%fused_computation.15.clone | custom fusion | bytes 3670048 | tf_op jit(solution)/shard_map/jit(_take)/gather | solution.py:60
  114.6 3.1 %fusion.91 = f32[128,2048]{0,1:T(8,128)S(1)} fusion(bf16[128,896,128]{2,1,0:T(8,128)(2,1)} %param.12, bf16[8,128,896]{2,1,0:T(8,128)(2,1)} %gather_fusion, pred[8]{0:T(512)(128)(4,1)S(1)} %copy-done.28), kind=kOutput, calls=%fused_computation.112 | convolution fusion | flops 235798528 | bytes 3735560 | tf_op jit(solution)/shard_map/dot_general | solution.py:61
  117.7 2.6 %fusion.101 = f32[128,2048]{0,1:T(8,128)S(1)} fusion(f32[128,2048]{0,1:T(8,128)S(1)} %fusion.91, bf16[128,896,128]{2,1,0:T(8,128)(2,1)} %param.12, bf16[8,128,896]{2,1,0:T(8,128)(2,1)S(1)} %copy-done.16, pred[8]{0:T(512)(128)(4,1)S(1)} %copy-done.27), kind=kOutput, calls=%fused_computation.114 | convolution fusion | flops 235798528 | bytes 3736064 | tf_op jit(solution)/shard_map/dot_general | solution.py:61
  120.4 2.7 %fusion.111 = f32[128,2048]{0,1:T(8,128)S(1)} fusion(f32[128,2048]{0,1:T(8,128)S(1)} %fusion.101, bf16[128,896,128]{2,1,0:T(8,128)(2,1)} %param.12, bf16[8,128,896]{2,1,0:T(8,128)(2,1)S(1)} %copy-done.15, pred[8]{0:T(512)(128)(4,1)S(1)} %copy-done.26), kind=kOutput, calls=%fused_computation.116 | convolution fusion | flops 235798528 | bytes 3736064 | tf_op jit(solution)/shard_map/dot_general | solution.py:61
  123.1 2.6 %fusion.121 = f32[128,2048]{0,1:T(8,128)S(1)} fusion(f32[128,2048]{0,1:T(8,128)S(1)} %fusion.111, bf16[128,896,128]{2,1,0:T(8,128)(2,1)} %param.12, bf16[8,128,896]{2,1,0:T(8,128)(2,1)S(1)} %copy-done.14, pred[8]{0:T(512)(128)(4,1)S(1)} %copy-done.25), kind=kOutput, calls=%fused_computation.118 | convolution fusion | flops 235798528 | bytes 3736064 | tf_op jit(solution)/shard_map/dot_general | solution.py:61
  125.8 2.5 %fusion.131 = f32[128,2048]{0,1:T(8,128)S(1)} fusion(f32[128,2048]{0,1:T(8,128)S(1)} %fusion.121, bf16[128,896,128]{2,1,0:T(8,128)(2,1)} %param.12, bf16[8,128,896]{2,1,0:T(8,128)(2,1)S(1)} %copy-done.13, pred[8]{0:T(512)(128)(4,1)S(1)} %copy-done.24), kind=kOutput, calls=%fused_computation.120 | convolution fusion | flops 235798528 | bytes 3736064 | tf_op jit(solution)/shard_map/dot_general | solution.py:61
  128.3 2.6 %fusion.141 = f32[128,2048]{0,1:T(8,128)S(1)} fusion(f32[128,2048]{0,1:T(8,128)S(1)} %fusion.131, bf16[128,896,128]{2,1,0:T(8,128)(2,1)} %param.12, bf16[8,128,896]{2,1,0:T(8,128)(2,1)S(1)} %copy-done.12, pred[8]{0:T(512)(128)(4,1)S(1)} %copy-done.23), kind=kOutput, calls=%fused_computation.122 | convolution fusion | flops 235798528 | bytes 3736064 | tf_op jit(solution)/shard_map/dot_general | solution.py:61
  130.9 2.5 %fusion.151 = f32[128,2048]{0,1:T(8,128)S(1)} fusion(f32[128,2048]{0,1:T(8,128)S(1)} %fusion.141, bf16[128,896,128]{2,1,0:T(8,128)(2,1)} %param.12, bf16[8,128,896]{2,1,0:T(8,128)(2,1)S(1)} %copy-done.11, pred[8]{0:T(512)(128)(4,1)S(1)} %copy-done.22), kind=kOutput, calls=%fused_computation.124 | convolution fusion | flops 235798528 | bytes 3736064 | tf_op jit(solution)/shard_map/dot_general | solution.py:61
  133.5 2.6 %fusion.161 = f32[128,2048]{0,1:T(8,128)S(1)} fusion(f32[128,2048]{0,1:T(8,128)S(1)} %fusion.151, bf16[128,896,128]{2,1,0:T(8,128)(2,1)} %param.12, bf16[8,128,896]{2,1,0:T(8,128)(2,1)S(1)} %copy-done.10, pred[8]{0:T(512)(128)(4,1)S(1)} %copy-done.21), kind=kOutput, calls=%fused_computation.126 | convolution fusion | flops 235798528 | bytes 3736064 | tf_op jit(solution)/shard_map/dot_general | solution.py:61
  136.1 2.5 %fusion.171 = f32[128,2048]{0,1:T(8,128)S(1)} fusion(f32[128,2048]{0,1:T(8,128)S(1)} %fusion.161, bf16[128,896,128]{2,1,0:T(8,128)(2,1)} %param.12, bf16[8,128,896]{2,1,0:T(8,128)(2,1)S(1)} %copy-done.9, pred[8]{0:T(512)(128)(4,1)S(1)} %copy-done.20), kind=kOutput, calls=%fused_computation.128 | convolution fusion | flops 235798528 | bytes 3736064 | tf_op jit(solution)/shard_map/dot_general | solution.py:61
  138.7 2.6 %fusion.181 = f32[128,2048]{0,1:T(8,128)S(1)} fusion(f32[128,2048]{0,1:T(8,128)S(1)} %fusion.171, bf16[128,896,128]{2,1,0:T(8,128)(2,1)} %param.12, bf16[8,128,896]{2,1,0:T(8,128)(2,1)S(1)} %copy-done.8, pred[8]{0:T(512)(128)(4,1)S(1)} %copy-done.19), kind=kOutput, calls=%fused_computation.130 | convolution fusion | flops 235798528 | bytes 3736064 | tf_op jit(solution)/shard_map/dot_general | solution.py:61
  141.3 2.5 %fusion.191 = f32[128,2048]{0,1:T(8,128)S(1)} fusion(f32[128,2048]{0,1:T(8,128)S(1)} %fusion.181, bf16[128,896,128]{2,1,0:T(8,128)(2,1)} %param.12, bf16[8,128,896]{2,1,0:T(8,128)(2,1)S(1)} %copy-done.7, pred[8]{0:T(512)(128)(4,1)S(1)} %copy-done.18), kind=kOutput, calls=%fused_computation.132 | convolution fusion | flops 235798528 | bytes 3736064 | tf_op jit(solution)/shard_map/dot_general | solution.py:61
  143.9 2.6 %fusion.201 = f32[128,2048]{0,1:T(8,128)S(1)} fusion(f32[128,2048]{0,1:T(8,128)S(1)} %fusion.191, bf16[128,896,128]{2,1,0:T(8,128)(2,1)} %param.12, bf16[8,128,896]{2,1,0:T(8,128)(2,1)S(1)} %copy-done.6, pred[8]{0:T(512)(128)(4,1)S(1)} %get-tuple-element.44), kind=kOutput, calls=%fused_computation.134 | convolution fusion | flops 235798528 | bytes 3736064 | tf_op jit(solution)/shard_map/dot_general | solution.py:61
  146.4 2.5 %fusion.211 = f32[128,2048]{0,1:T(8,128)S(1)} fusion(f32[128,2048]{0,1:T(8,128)S(1)} %fusion.201, bf16[128,896,128]{2,1,0:T(8,128)(2,1)} %param.12, bf16[8,128,896]{2,1,0:T(8,128)(2,1)S(1)} %copy-done.5, pred[8]{0:T(512)(128)(4,1)S(1)} %get-tuple-element.42), kind=kOutput, calls=%fused_computation.136 | convolution fusion | flops 235798528 | bytes 3736064 | tf_op jit(solution)/shard_map/dot_general | solution.py:61
  149.0 2.6 %fusion.221 = f32[128,2048]{0,1:T(8,128)S(1)} fusion(f32[128,2048]{0,1:T(8,128)S(1)} %fusion.211, bf16[128,896,128]{2,1,0:T(8,128)(2,1)} %param.12, bf16[8,128,896]{2,1,0:T(8,128)(2,1)S(1)} %copy-done.4, pred[8]{0:T(512)(128)(4,1)S(1)} %get-tuple-element.40), kind=kOutput, calls=%fused_computation.138 | convolution fusion | flops 235798528 | bytes 3736064 | tf_op jit(solution)/shard_map/dot_general | solution.py:61
  151.6 2.5 %fusion.231 = f32[128,2048]{0,1:T(8,128)S(1)} fusion(f32[128,2048]{0,1:T(8,128)S(1)} %fusion.221, bf16[128,896,128]{2,1,0:T(8,128)(2,1)} %param.12, bf16[8,128,896]{2,1,0:T(8,128)(2,1)S(1)} %copy-done.3, pred[8]{0:T(512)(128)(4,1)S(1)} %get-tuple-element.68), kind=kOutput, calls=%fused_computation.140 | convolution fusion | flops 235798528 | bytes 3736064 | tf_op jit(solution)/shard_map/dot_general | solution.py:61
  154.1 2.6 %fusion.241 = f32[128,2048]{0,1:T(8,128)S(1)} fusion(f32[128,2048]{0,1:T(8,128)S(1)} %fusion.231, bf16[128,896,128]{2,1,0:T(8,128)(2,1)} %param.12, bf16[8,128,896]{2,1,0:T(8,128)(2,1)S(1)} %copy-done.2, pred[8]{0:T(512)(128)(4,1)S(1)} %get-tuple-element.6), kind=kOutput, calls=%fused_computation.142 | convolution fusion | flops 235798528 | bytes 3736064 | tf_op jit(solution)/shard_map/dot_general | solution.py:61
  156.7 0.7 fusion.289
  157.5 1.3 collective-permute-start.1
  158.8 4.7 %collective-permute-start = (bf16[16,2048]{1,0:T(8,128)(2,1)S(1)}, bf16[16,2048]{1,0:T(8,128)(2,1)S(1)}, u32[]{:S(2)}, u32[]{:S(2)}) collective-permute-start(bf16[16,2048]{1,0:T(8,128)(2,1)S(1)} %get-tuple-element.38), channel_id=1, source_target_pairs={{0,16},{16,32},{32,48},{48,64},{64,80},{80,96},{96,112},{112,128},... | collective-permute-start | bytes 196616 | tf_op jit(solution)/shard_map/ppermute | solution.py:22
  163.4 1.3 collective-permute-done
  164.9 18.6 %all_to_all.16 = f32[16,2,2048]{2,1,0:T(2,128)S(1)} all-to-all(f32[16,2,2048]{2,1,0:T(2,128)S(1)} %reshape.161), channel_id=1, replica_groups=mesh['gz'=16,'ang'=16] {'ang'}, dimensions={0} | all-to-all | bytes 524288 | tf_op jit(solution)/shard_map/all_to_all | solution.py:32
  (86 shorter events, 5.5 us)
Async XLA Ops:
  0.0 13.2 %copy-start = (bf16[896,896]{1,0:T(8,128)(2,1)S(1)}, bf16[896,896]{1,0:T(8,128)(2,1)}, u32[]{:S(2)}) copy-start(bf16[896,896]{1,0:T(8,128)(2,1)} %param.9) | copy-start | bytes 4816900
  3.1 17.4 %all-to-all-start = ((s32[16,1,2]{2,1,0:T(1,128)}), s32[16,1,2]{2,1,0:T(1,128)S(1)}, u32[]{:S(2)}, u32[]{:S(2)}) async-start(s32[16,1,2]{2,1,0:T(1,128)} %bitcast.2), calls=%async_computation | async-start | bytes 16384 | tf_op jit(solution)/shard_map/all_to_all | solution.py:84
  20.5 7.7 %copy-start.17 = (s32[128]{0:T(128)S(1)}, s32[128]{0:T(128)}, u32[]{:S(2)}) copy-start(s32[128]{0:T(128)} %param.13) | copy-start | bytes 1540
  20.5 49.2 %all-to-all-start.1 = ((bf16[16,2,32,896]{3,2,1,0:T(8,128)(2,1)}), bf16[16,2,32,896]{3,2,1,0:T(8,128)(2,1)S(1)}, u32[]{:S(2)}, u32[]{:S(2)}) async-start(bf16[16,2,32,896]{3,2,1,0:T(8,128)(2,1)} %bitcast.40), calls=%async_computation.1 | async-start | bytes 3670016 | tf_op jit(solution)/shard_map/all_to_all | solution.py:83
  112.7 2.0 %copy-start.28 = (pred[8]{0:T(512)(128)(4,1)S(1)}, pred[8]{0:T(512)(128)(4,1)}, u32[]{:S(2)}) copy-start(pred[8]{0:T(512)(128)(4,1)} %get-tuple-element.66) | copy-start | bytes 28
  114.6 3.1 %copy-start.16 = (bf16[8,128,896]{2,1,0:T(8,128)(2,1)S(1)}, bf16[8,128,896]{2,1,0:T(8,128)(2,1)}, u32[]{:S(2)}) copy-start(bf16[8,128,896]{2,1,0:T(8,128)(2,1)} %gather_fusion.1) | copy-start | bytes 5505028
  114.6 3.1 %copy-start.27 = (pred[8]{0:T(512)(128)(4,1)S(1)}, pred[8]{0:T(512)(128)(4,1)}, u32[]{:S(2)}) copy-start(pred[8]{0:T(512)(128)(4,1)} %get-tuple-element.64) | copy-start | bytes 28
  117.7 2.6 %copy-start.15 = (bf16[8,128,896]{2,1,0:T(8,128)(2,1)S(1)}, bf16[8,128,896]{2,1,0:T(8,128)(2,1)}, u32[]{:S(2)}) copy-start(bf16[8,128,896]{2,1,0:T(8,128)(2,1)} %gather_fusion.2) | copy-start | bytes 5505028
  117.7 2.6 %copy-start.26 = (pred[8]{0:T(512)(128)(4,1)S(1)}, pred[8]{0:T(512)(128)(4,1)}, u32[]{:S(2)}) copy-start(pred[8]{0:T(512)(128)(4,1)} %get-tuple-element.62) | copy-start | bytes 28
  120.3 2.8 %copy-start.14 = (bf16[8,128,896]{2,1,0:T(8,128)(2,1)S(1)}, bf16[8,128,896]{2,1,0:T(8,128)(2,1)}, u32[]{:S(2)}) copy-start(bf16[8,128,896]{2,1,0:T(8,128)(2,1)} %gather_fusion.3) | copy-start | bytes 5505028
  120.4 2.8 %copy-start.25 = (pred[8]{0:T(512)(128)(4,1)S(1)}, pred[8]{0:T(512)(128)(4,1)}, u32[]{:S(2)}) copy-start(pred[8]{0:T(512)(128)(4,1)} %get-tuple-element.60) | copy-start | bytes 28
  123.1 2.6 %copy-start.13 = (bf16[8,128,896]{2,1,0:T(8,128)(2,1)S(1)}, bf16[8,128,896]{2,1,0:T(8,128)(2,1)}, u32[]{:S(2)}) copy-start(bf16[8,128,896]{2,1,0:T(8,128)(2,1)} %gather_fusion.4) | copy-start | bytes 5505028
  123.1 2.6 %copy-start.24 = (pred[8]{0:T(512)(128)(4,1)S(1)}, pred[8]{0:T(512)(128)(4,1)}, u32[]{:S(2)}) copy-start(pred[8]{0:T(512)(128)(4,1)} %get-tuple-element.58) | copy-start | bytes 28
  125.7 2.5 %copy-start.12 = (bf16[8,128,896]{2,1,0:T(8,128)(2,1)S(1)}, bf16[8,128,896]{2,1,0:T(8,128)(2,1)}, u32[]{:S(2)}) copy-start(bf16[8,128,896]{2,1,0:T(8,128)(2,1)} %gather_fusion.5) | copy-start | bytes 5505028
  125.8 2.5 %copy-start.23 = (pred[8]{0:T(512)(128)(4,1)S(1)}, pred[8]{0:T(512)(128)(4,1)}, u32[]{:S(2)}) copy-start(pred[8]{0:T(512)(128)(4,1)} %get-tuple-element.56) | copy-start | bytes 28
  128.3 2.6 %copy-start.11 = (bf16[8,128,896]{2,1,0:T(8,128)(2,1)S(1)}, bf16[8,128,896]{2,1,0:T(8,128)(2,1)}, u32[]{:S(2)}) copy-start(bf16[8,128,896]{2,1,0:T(8,128)(2,1)} %gather_fusion.6) | copy-start | bytes 5505028
  128.3 2.6 %copy-start.22 = (pred[8]{0:T(512)(128)(4,1)S(1)}, pred[8]{0:T(512)(128)(4,1)}, u32[]{:S(2)}) copy-start(pred[8]{0:T(512)(128)(4,1)} %get-tuple-element.54) | copy-start | bytes 28
  130.9 2.5 %copy-start.10 = (bf16[8,128,896]{2,1,0:T(8,128)(2,1)S(1)}, bf16[8,128,896]{2,1,0:T(8,128)(2,1)}, u32[]{:S(2)}) copy-start(bf16[8,128,896]{2,1,0:T(8,128)(2,1)} %gather_fusion.7) | copy-start | bytes 5505028
  130.9 2.5 %copy-start.21 = (pred[8]{0:T(512)(128)(4,1)S(1)}, pred[8]{0:T(512)(128)(4,1)}, u32[]{:S(2)}) copy-start(pred[8]{0:T(512)(128)(4,1)} %get-tuple-element.52) | copy-start | bytes 28
  133.5 2.6 %copy-start.9 = (bf16[8,128,896]{2,1,0:T(8,128)(2,1)S(1)}, bf16[8,128,896]{2,1,0:T(8,128)(2,1)}, u32[]{:S(2)}) copy-start(bf16[8,128,896]{2,1,0:T(8,128)(2,1)} %gather_fusion.8) | copy-start | bytes 5505028
  133.5 2.6 %copy-start.20 = (pred[8]{0:T(512)(128)(4,1)S(1)}, pred[8]{0:T(512)(128)(4,1)}, u32[]{:S(2)}) copy-start(pred[8]{0:T(512)(128)(4,1)} %get-tuple-element.50) | copy-start | bytes 28
  136.1 2.5 %copy-start.8 = (bf16[8,128,896]{2,1,0:T(8,128)(2,1)S(1)}, bf16[8,128,896]{2,1,0:T(8,128)(2,1)}, u32[]{:S(2)}) copy-start(bf16[8,128,896]{2,1,0:T(8,128)(2,1)} %gather_fusion.9) | copy-start | bytes 5505028
  136.1 2.5 %copy-start.19 = (pred[8]{0:T(512)(128)(4,1)S(1)}, pred[8]{0:T(512)(128)(4,1)}, u32[]{:S(2)}) copy-start(pred[8]{0:T(512)(128)(4,1)} %get-tuple-element.48) | copy-start | bytes 28
  138.7 2.6 %copy-start.7 = (bf16[8,128,896]{2,1,0:T(8,128)(2,1)S(1)}, bf16[8,128,896]{2,1,0:T(8,128)(2,1)}, u32[]{:S(2)}) copy-start(bf16[8,128,896]{2,1,0:T(8,128)(2,1)} %gather_fusion.10) | copy-start | bytes 5505028
  138.7 2.6 %copy-start.18 = (pred[8]{0:T(512)(128)(4,1)S(1)}, pred[8]{0:T(512)(128)(4,1)}, u32[]{:S(2)}) copy-start(pred[8]{0:T(512)(128)(4,1)} %get-tuple-element.46) | copy-start | bytes 28
  141.3 2.5 %copy-start.6 = (bf16[8,128,896]{2,1,0:T(8,128)(2,1)S(1)}, bf16[8,128,896]{2,1,0:T(8,128)(2,1)}, u32[]{:S(2)}) copy-start(bf16[8,128,896]{2,1,0:T(8,128)(2,1)} %gather_fusion.11) | copy-start | bytes 5505028
  143.8 2.6 %copy-start.5 = (bf16[8,128,896]{2,1,0:T(8,128)(2,1)S(1)}, bf16[8,128,896]{2,1,0:T(8,128)(2,1)}, u32[]{:S(2)}) copy-start(bf16[8,128,896]{2,1,0:T(8,128)(2,1)} %gather_fusion.12) | copy-start | bytes 5505028
  146.4 2.5 %copy-start.4 = (bf16[8,128,896]{2,1,0:T(8,128)(2,1)S(1)}, bf16[8,128,896]{2,1,0:T(8,128)(2,1)}, u32[]{:S(2)}) copy-start(bf16[8,128,896]{2,1,0:T(8,128)(2,1)} %gather_fusion.13) | copy-start | bytes 5505028
  149.0 2.6 %copy-start.3 = (bf16[8,128,896]{2,1,0:T(8,128)(2,1)S(1)}, bf16[8,128,896]{2,1,0:T(8,128)(2,1)}, u32[]{:S(2)}) copy-start(bf16[8,128,896]{2,1,0:T(8,128)(2,1)} %gather_fusion.14) | copy-start | bytes 5505028
  151.6 2.5 %copy-start.2 = (bf16[8,128,896]{2,1,0:T(8,128)(2,1)S(1)}, bf16[8,128,896]{2,1,0:T(8,128)(2,1)}, u32[]{:S(2)}) copy-start(bf16[8,128,896]{2,1,0:T(8,128)(2,1)} %gather_fusion.15) | copy-start | bytes 5505028
  154.1 30.0 %copy-start.1 = (bf16[896,896]{1,0:T(8,128)(2,1)S(1)}, bf16[896,896]{1,0:T(8,128)(2,1)}, u32[]{:S(2)}) copy-start(bf16[896,896]{1,0:T(8,128)(2,1)} %param.9) | copy-start | bytes 4816900
  157.5 6.0 %collective-permute-start.1 = (bf16[16,2048]{1,0:T(8,128)(2,1)S(1)}, bf16[16,2048]{1,0:T(8,128)(2,1)S(1)}, u32[]{:S(2)}, u32[]{:S(2)}) collective-permute-start(bf16[16,2048]{1,0:T(8,128)(2,1)S(1)} %get-tuple-element.39), channel_id=1, source_target_pairs={{16,0},{32,16},{48,32},{64,48},{80,64},{96,80},{112,96},{128,112},... | collective-permute-start | bytes 196616 | tf_op jit(solution)/shard_map/ppermute | solution.py:22
  158.8 6.0 %collective-permute-start = (bf16[16,2048]{1,0:T(8,128)(2,1)S(1)}, bf16[16,2048]{1,0:T(8,128)(2,1)S(1)}, u32[]{:S(2)}, u32[]{:S(2)}) collective-permute-start(bf16[16,2048]{1,0:T(8,128)(2,1)S(1)} %get-tuple-element.38), channel_id=1, source_target_pairs={{0,16},{16,32},{32,48},{48,64},{64,80},{80,96},{96,112},{112,128},... | collective-permute-start | bytes 196616 | tf_op jit(solution)/shard_map/ppermute | solution.py:22
where the time goes:
time: 187 us; the launch traced here: 184 us
  matrix products  57.1 us (31%)
  local copies, waits for them, and re-layouts  38.9 us (21%)
  waiting for transfers between devices  26 us (14%)
  starting transfers between devices  23.7 us (13%)
  other arithmetic  19.2 us (10%)
  blocking collectives  18.6 us (10%)
    dot_general x16, matrix products, backproject(): jnp.dot(chosen, weights[pixel_block], preferred_element_type=jnp.float32)  41.4 us
    gather x16, local copies, waits for them, and re-layouts, backproject(): jnp.take(filtered, view_order[pixel_block], axis=1)  32.2 us
    all_to_all x1, waiting for transfers between devices, row_route(): lax.all_to_all(packed, 'gz', split_axis=0, concat_axis=0, tiled=True)  24.6 us
    all_to_all x1, blocking collectives, summed_on_arrival(): lax.all_to_all(in_blocks(shard, dim, devices), axis, 0, 0, tiled=True)  18.6 us
    another operation x1, other arithmetic  14.5 us
    dot_general x1, matrix products, ramp_filter(): lax.dot_general(weighted, dft_table, (((1,), (1,)), ((), ())), preferred_...  10.9 us
    all_to_all x1, starting transfers between devices, row_route(): lax.all_to_all(slot_offset, 'gz', split_axis=0, concat_axis=0, tiled=True)  10.1 us
    all_to_all x1, starting transfers between devices, row_route(): lax.all_to_all(packed, 'gz', split_axis=0, concat_axis=0, tiled=True)  7.62 us
  transfers between devices with their start and end apart: 4, of which 3 were waited for; matrix products, arithmetic and copies ran while one was open for 13% of the time, Pallas kernels for 0%

commit v1 on v0

v1 whole, which is shorter than its diff:
```python
import functools
import math

import jax
import jax.numpy as jnp
import ml_dtypes
import numpy as np
from jax import lax
from jax.experimental import pallas as pl
from jax.experimental.pallas import tpu as pltpu
from jax.sharding import PartitionSpec as P

BR = 4
TILE_PIX = 128
F32, BF16 = jnp.float32, jnp.bfloat16


def filter_operator(columns):
    index = np.arange(columns)
    radians = (index[:, None] * index[None, :] % columns).astype(np.float64) * (2.0 * math.pi / columns)
    table = np.concatenate([np.cos(radians), np.sin(radians)], axis=1)
    table = table.astype(np.float32).astype(ml_dtypes.bfloat16).astype(np.float64)
    frequency = np.minimum(index, columns - index) * (2.0 / (columns * columns))
    ramp = np.concatenate([frequency, frequency])
    return ((table * ramp) @ table.T).astype(np.float32).astype(ml_dtypes.bfloat16)


def kernel(
    n_gz, n_ang,
    slab_ref, offset_ref, view_ref, fan_hbm, rebin_hbm, filter_hbm, tiles_hbm,
    out_ref,
    fan_v, rebin_v, filter_v, tiles_v, par_v, filt_v, place_v,
    send1, recv1, send2, recv2, send3, recv3,
    in_sem, tile_sem, s1, r1, s2, r2, s3, r3,
):
    gz, ang = lax.axis_index("gz"), lax.axis_index("ang")
    blocks, views, rows, cols = n_ang, fan_v.shape[1], fan_v.shape[0], fan_v.shape[2]
    zd = send2.shape[1]
    total_z = n_gz * zd

    def ang_peer(d):
        return lax.rem(ang + d, n_ang)

    def gz_peer(d):
        return lax.rem(gz + d, n_gz)

    loads = [
        pltpu.make_async_copy(fan_hbm.at[0], fan_v, in_sem.at[0]),
        pltpu.make_async_copy(rebin_hbm, rebin_v, in_sem.at[1]),
        pltpu.make_async_copy(filter_hbm, filter_v, in_sem.at[2]),
    ]
    for load in loads:
        load.start()

    def tile_load(i):
        return pltpu.make_async_copy(
            tiles_hbm.at[pl.ds(ang_peer(i + 1) * views, views)],
            tiles_v.at[pl.ds(i * views, views)],
            tile_sem.at[i],
        )

    def start_tile(i, carry):
        tile_load(i).start()
        return carry

    lax.fori_loop(0, blocks, start_tile, 0)

    barrier = pltpu.get_barrier_semaphore()
    for d in range(1, n_ang):
        pl.semaphore_signal(barrier, inc=1, device_id={"ang": ang_peer(d)}, device_id_type=pl.DeviceIdType.MESH)
    for d in range(1, n_gz):
        pl.semaphore_signal(barrier, inc=1, device_id={"gz": gz_peer(d)}, device_id_type=pl.DeviceIdType.MESH)

    lane = lax.broadcasted_iota(jnp.int32, (1, 2 * rows), 1)
    lane = lax.rem(lane, rows)
    depth = jnp.full((1, 2 * rows), -1, jnp.int32)
    for b in range(rows // BR):
        first = slab_ref[0, b] * zd + offset_ref[0, b] - zd // 2
        depth = jnp.where(lane // BR == b, first + lax.rem(lane, BR), depth)
    slices = lax.broadcasted_iota(jnp.int32, (total_z, 2 * rows), 0)
    place_v[...] = jnp.where(slices == depth, 1.0, 0.0).astype(BF16)

    loads[0].wait()
    loads[1].wait()
    par = jnp.dot(fan_v[...].reshape(rows * views, cols), rebin_v[...], preferred_element_type=F32)
    for c in range(cols // 128):
        par_v[c * rows * views : (c + 1) * rows * views] = par[:, c * 128 : (c + 1) * 128]
    loads[2].wait()
    by_view = jnp.concatenate(
        [
            jnp.concatenate(
                [par_v[pl.ds(c * rows * views + v, rows, stride=views)].astype(BF16) for c in range(cols // 128)],
                axis=1,
            )
            for v in range(views)
        ],
        axis=0,
    )
    filtered = jnp.dot(by_view, filter_v[...], preferred_element_type=F32).astype(BF16)
    filt_v[...] = filtered.reshape(views, rows, cols)

    pl.semaphore_wait(barrier, n_ang + n_gz - 2)

    def send_partial(i):
        to = ang_peer(i + 1)
        return pltpu.make_async_remote_copy(
            src_ref=send1.at[i], dst_ref=recv1.at[ang], send_sem=s1.at[i], recv_sem=r1.at[ang],
            device_id={"ang": to}, device_id_type=pl.DeviceIdType.MESH,
        )

    def pair(k, carry):
        a, b = 2 * k, 2 * k + 1
        tile_load(a).wait()
        tile_load(b).wait()
        acc = jnp.zeros((2 * rows, 2 * TILE_PIX), F32)
        for j in range(0, views, 2):
            lhs = jnp.concatenate(
                [
                    jnp.concatenate(
                        [filt_v[view_ref[ang_peer(x + 1) * views + j + h]] for h in range(2)], axis=1
                    )
                    for x in (a, b)
                ],
                axis=0,
            )
            rhs = jnp.concatenate(
                [
                    jnp.concatenate([tiles_v[x * views + j + h] for h in range(2)], axis=0)
                    for x in (a, b)
                ],
                axis=1,
            )
            acc = acc + jnp.dot(lhs, rhs, preferred_element_type=F32)
        send1[a] = acc[:rows, :TILE_PIX].astype(BF16)
        send1[b] = acc[rows:, TILE_PIX:].astype(BF16)
        send_partial(a).start()

        @pl.when(b < blocks - 1)
        def _():
            send_partial(b).start()

        return carry

    lax.fori_loop(0, blocks // 2, pair, 0)

    def wait_recv(buffer, sem, index, axis):
        pltpu.make_async_remote_copy(
            src_ref=buffer.at[index], dst_ref=buffer.at[index], send_sem=sem.at[index], recv_sem=sem.at[index],
            device_id={axis: index}, device_id_type=pl.DeviceIdType.MESH,
        ).wait_recv()

    for d in range(1, n_ang):
        wait_recv(recv1, r1, ang_peer(d), "ang")
    total = send1[blocks - 1].astype(F32)
    for d in range(1, n_ang):
        total = total + recv1[ang_peer(d)].astype(F32)
    high = total.astype(BF16)
    low = (total - high.astype(F32)).astype(BF16)
    placed = jnp.dot(place_v[...], jnp.concatenate([high, low], axis=0), preferred_element_type=F32)
    send2[...] = placed.astype(BF16).reshape(n_gz, zd, TILE_PIX)

    def send_slab(d):
        to = gz_peer(d)
        return pltpu.make_async_remote_copy(
            src_ref=send2.at[to], dst_ref=recv2.at[gz], send_sem=s2.at[to], recv_sem=r2.at[gz],
            device_id={"gz": to}, device_id_type=pl.DeviceIdType.MESH,
        )

    for d in range(1, n_gz):
        send_slab(d).start()
    slab = send2[gz].astype(F32)
    for d in range(1, n_gz):
        wait_recv(recv2, r2, gz_peer(d), "gz")
    for d in range(1, n_gz):
        slab = slab + recv2[gz_peer(d)].astype(F32)

    send3[...] = slab.reshape(n_ang, 2, TILE_PIX)

    def send_slices(d):
        to = ang_peer(d)
        return pltpu.make_async_remote_copy(
            src_ref=send3.at[to], dst_ref=recv3.at[ang], send_sem=s3.at[to], recv_sem=r3.at[ang],
            device_id={"ang": to}, device_id_type=pl.DeviceIdType.MESH,
        )

    for d in range(1, n_ang):
        send_slices(d).start()
    recv3[ang] = send3[ang]
    for d in range(1, n_ang):
        wait_recv(recv3, r3, ang_peer(d), "ang")
    for p in range(blocks):
        out_ref[:, p * TILE_PIX : (p + 1) * TILE_PIX] = recv3[p]

    for i in range(blocks - 1):
        send_partial(i).wait_send()
    for d in range(1, n_gz):
        send_slab(d).wait_send()
    for d in range(1, n_ang):
        send_slices(d).wait_send()


def on_device(n_gz, n_ang, fan_views, rebin_weight, slab_table, slice_offset, tiles, tile_view):
    _, rows, views, cols = fan_views.shape
    zd = 2 * n_ang
    operator = jnp.asarray(filter_operator(cols))
    dma = pltpu.SemaphoreType.DMA
    smem, hbm = pl.BlockSpec(memory_space=pltpu.SMEM), pl.BlockSpec(memory_space=pl.ANY)
    return pl.pallas_call(
        functools.partial(kernel, n_gz, n_ang),
        out_shape=jax.ShapeDtypeStruct((2, n_ang * TILE_PIX), F32),
        in_specs=[smem, smem, smem, hbm, hbm, hbm, hbm],
        out_specs=pl.BlockSpec(memory_space=pltpu.VMEM),
        scratch_shapes=[
            pltpu.VMEM((rows, views, cols), BF16),
            pltpu.VMEM((cols, cols), BF16),
            pltpu.VMEM((cols, cols), BF16),
            pltpu.VMEM((n_ang * views, cols, TILE_PIX), BF16),
            pltpu.VMEM((cols // 128 * rows * views, 128), F32),
            pltpu.VMEM((views, rows, cols), BF16),
            pltpu.VMEM((n_gz * zd, 2 * rows), BF16),
            pltpu.VMEM((n_ang, rows, TILE_PIX), BF16),
            pltpu.VMEM((n_ang, rows, TILE_PIX), BF16),
            pltpu.VMEM((n_gz, zd, TILE_PIX), BF16),
            pltpu.VMEM((n_gz, zd, TILE_PIX), BF16),
            pltpu.VMEM((n_ang, 2, TILE_PIX), F32),
            pltpu.VMEM((n_ang, 2, TILE_PIX), F32),
            dma((3,)),
            dma((n_ang,)),
            dma((n_ang,)), dma((n_ang,)),
            dma((n_gz,)), dma((n_gz,)),
            dma((n_ang,)), dma((n_ang,)),
        ],
        compiler_params=pltpu.CompilerParams(
            collective_id=0, has_side_effects=True, vmem_limit_bytes=60 * 1024 * 1024
        ),
        name="reconstruct",
    )(slab_table[:, :, 0], slice_offset, tile_view, fan_views, rebin_weight, operator, tiles)


def solution(mesh):
    n_gz, n_ang = mesh.shape["gz"], mesh.shape["ang"]
    in_specs = (
        P("gz", None, "ang", None),
        P(),
        P("gz", None, None),
        P("gz", None),
        P("ang", None, None),
        P("ang"),
    )
    out_specs = P(("gz", "ang"), None)
    return jax.shard_map(
        functools.partial(on_device, n_gz, n_ang),
        mesh=mesh, in_specs=in_specs, out_specs=out_specs, check_vma=False,
    )
```

time: 187 us -> 37.1 us (0.20); the launches traced: 184 us -> 37 us
  matrix products: 57.1 us -> 0 us
  local copies, waits for them, and re-layouts: 38.9 us -> 1.32 us
  Pallas kernels: 0 us -> 35.6 us
  waiting for transfers between devices: 26 us -> 0 us
  starting transfers between devices: 23.7 us -> 0 us
  other arithmetic: 19.2 us -> 0 us
  blocking collectives: 18.6 us -> 0 us
    dot_general x20 -> x0, matrix products: 57.1 us -> none  [the longest x16 41.4 us: backproject(): jnp.dot(chosen, weights[pixel_block], preferred_element_type=jnp.float32)]
    pallas_call x0 -> x1, Pallas kernels: none -> 35.6 us  [on_device(): pl.pallas_call(functools.partial(kernel, n_gz, n_ang), out_shape=jax.Shap...]
    gather x16 -> x0, local copies, waits for them, and re-layouts: 32.2 us -> none  [backproject(): jnp.take(filtered, view_order[pixel_block], axis=1)]
    all_to_all x2 -> x0, waiting for transfers between devices: 24.7 us -> none  [the longest x1 24.6 us: row_route(): lax.all_to_all(packed, 'gz', split_axis=0, concat_axis=0, tiled=True)]
    all_to_all x1 -> x0, blocking collectives: 18.6 us -> none  [summed_on_arrival(): lax.all_to_all(in_blocks(shard, dim, devices), axis, 0, 0, tiled=True)]
    all_to_all x2 -> x0, starting transfers between devices: 17.7 us -> none  [the longest x1 10.1 us: row_route(): lax.all_to_all(slot_offset, 'gz', split_axis=0, concat_axis=0, tiled=True)]
    another operation x1 -> x0, other arithmetic: 14.5 us -> none
    ppermute x2 -> x0, starting transfers between devices: 5.95 us -> none  [from_behind(): return lax.ppermute(shard, axis, pairs)]
  transfers between devices with their start and end apart: 4 -> 0, of which waited for: 3 -> 0; matrix products, arithmetic and copies ran while one was open for 13% -> 0% of each run, Pallas kernels for 0% -> 0%
where the time goes in v1:
time: 37.1 us; the launch traced here: 37 us
  Pallas kernels  35.6 us (96%)
  local copies, waits for them, and re-layouts  1.32 us (4%)
    pallas_call x1, Pallas kernels, on_device(): pl.pallas_call(functools.partial(kernel, n_gz, n_ang), out_shape=jax.Shap...  35.6 us
    unnamed x1, local copies, waits for them, and re-layouts  1.32 us

profile of v1, /device:TPU:1, one launch (start us, length us, event | category | flops | bytes accessed | tf_op | source)
XLA Modules:
  0.0 37.0 jit_solution(1507143061380855614)
XLA Ops:
  0.0 35.6 %reconstruct.1 = f32[2,2048]{1,0:T(2,128)} custom-call(s32[1,16]{1,0:T(1,128)} %bitcast.1, s32[1,16]{1,0:T(1,128)} %offset_ref.1, s32[128]{0:T(128)} %view_ref.1, bf16[1,64,8,896]{3,2,1,0:T(8,128)(2,1)} %fan_hbm.1, bf16[896,896]{1,0:T(8,128)(2,1)} %rebin_hbm.1, bf16[896,896]{1,0:T(8,128)(2,1)} %constant.2.clone.filter_hbm, bf16[128,896,128]{2,1,0:T(8,128)(2,1)} %tiles_hbm.1), custom_call_target="tpu_custom_call" | custom-call | tf_op jit(solution)/shard_map/reconstruct/pallas_call | solution.py:208
  35.6 1.3 %copy.9 = f32[2,2048]{1,0:T(2,128)} copy(f32[2,2048]{1,0:T(2,128)} %reconstruct.1) | data formatting | bytes 32768

commit v2 on v1

v2 whole, which is shorter than its diff:
```python
import functools
import math

import jax
import jax.numpy as jnp
import ml_dtypes
import numpy as np
from jax import lax
from jax.experimental import pallas as pl
from jax.experimental.pallas import tpu as pltpu
from jax.sharding import PartitionSpec as P

BR = 4
TILE_PIX = 128
F32, BF16 = jnp.float32, jnp.bfloat16


def filter_operator(columns):
    index = np.arange(columns)
    radians = (index[:, None] * index[None, :] % columns).astype(np.float64) * (2.0 * math.pi / columns)
    table = np.concatenate([np.cos(radians), np.sin(radians)], axis=1)
    table = table.astype(np.float32).astype(ml_dtypes.bfloat16).astype(np.float64)
    frequency = np.minimum(index, columns - index) * (2.0 / (columns * columns))
    ramp = np.concatenate([frequency, frequency])
    return ((table * ramp) @ table.T).astype(np.float32).astype(ml_dtypes.bfloat16)


def kernel(
    n_gz, n_ang,
    slab_hbm, offset_hbm, view_hbm, fan_hbm, rebin_hbm, filter_hbm, tiles_hbm,
    out_ref,
    fan_v, rebin_v, filter_v, tiles_v, par_v, filt_v, place_v,
    send1, recv1, send2, recv2, slab_ref, offset_ref, view_ref,
    in_sem, tile_sem, s1, r1, s2, r2,
):
    gz, ang = lax.axis_index("gz"), lax.axis_index("ang")
    blocks, views, rows, cols = n_ang, fan_v.shape[1], fan_v.shape[0], fan_v.shape[2]
    zd = 2 * n_ang
    total_z = n_gz * zd

    def ang_at(dx, dy, dc):
        x, y, c = ang // 4, lax.rem(ang // 2, 2), lax.rem(ang, 2)
        return lax.rem(x + dx, 4) * 4 + lax.rem(y + dy, 2) * 2 + lax.rem(c + dc, 2)

    def gz_at(dy, dz):
        length = n_gz // 2
        y, z = gz // length, lax.rem(gz, length)
        return lax.rem(y + dy, 2) * length + lax.rem(z + dz, length)

    ang_order = [
        ang_at(dx, dy, dc)
        for dx, dy in ((2, 1), (1, 1), (3, 1), (2, 0), (0, 1), (1, 0), (3, 0), (0, 0))
        for dc in (1, 0)
    ]
    length = n_gz // 2
    gz_order = sorted(
        [(dy, dz) for dy in range(2) for dz in range(length)],
        key=lambda at: -at[0] - min(at[1], length - at[1]),
    )

    def ang_peer(d):
        return lax.rem(ang + d, n_ang)

    def gz_peer(d):
        return lax.rem(gz + d, n_gz)

    loads = [
        pltpu.make_async_copy(fan_hbm.at[0], fan_v, in_sem.at[0]),
        pltpu.make_async_copy(rebin_hbm, rebin_v, in_sem.at[1]),
        pltpu.make_async_copy(filter_hbm, filter_v, in_sem.at[2]),
        pltpu.make_async_copy(slab_hbm, slab_ref, in_sem.at[3]),
        pltpu.make_async_copy(offset_hbm, offset_ref, in_sem.at[4]),
        pltpu.make_async_copy(view_hbm, view_ref, in_sem.at[5]),
    ]
    for load in loads:
        load.start()

    def tile_load(i):
        return pltpu.make_async_copy(
            tiles_hbm.at[pl.ds(ang_order[i] * views, views)],
            tiles_v.at[pl.ds(i * views, views)],
            tile_sem.at[i],
        )

    for i in range(blocks):
        tile_load(i).start()

    barrier = pltpu.get_barrier_semaphore()
    for d in range(1, n_ang):
        pl.semaphore_signal(barrier, inc=1, device_id={"ang": ang_peer(d)}, device_id_type=pl.DeviceIdType.MESH)
    for d in range(1, n_gz):
        pl.semaphore_signal(barrier, inc=1, device_id={"gz": gz_peer(d)}, device_id_type=pl.DeviceIdType.MESH)

    for load in loads[3:]:
        load.wait()
    lane = lax.broadcasted_iota(jnp.int32, (1, 2 * rows), 1)
    lane = lax.rem(lane, rows)
    depth = jnp.full((1, 2 * rows), -1, jnp.int32)
    for b in range(rows // BR):
        first = slab_ref[0, b] * zd + offset_ref[0, b] - zd // 2
        depth = jnp.where(lane // BR == b, first + lax.rem(lane, BR), depth)
    slices = lax.broadcasted_iota(jnp.int32, (total_z, 2 * rows), 0)
    place_v[...] = jnp.where(slices == depth, 1.0, 0.0).astype(BF16)

    loads[0].wait()
    loads[1].wait()
    par = jnp.dot(fan_v[...].reshape(rows * views, cols), rebin_v[...], preferred_element_type=F32)
    for c in range(cols // 128):
        par_v[c * rows * views : (c + 1) * rows * views] = par[:, c * 128 : (c + 1) * 128]
    loads[2].wait()
    by_view = jnp.concatenate(
        [
            jnp.concatenate(
                [par_v[pl.ds(c * rows * views + v, rows, stride=views)].astype(BF16) for c in range(cols // 128)],
                axis=1,
            )
            for v in range(views)
        ],
        axis=0,
    )
    filtered = jnp.dot(by_view, filter_v[...], preferred_element_type=F32).astype(BF16)
    filt_v[...] = filtered.reshape(views, rows, cols)

    def send_partial(i):
        return pltpu.make_async_remote_copy(
            src_ref=send1.at[i], dst_ref=recv1.at[ang], send_sem=s1.at[i], recv_sem=r1.at[ang],
            device_id={"ang": ang_order[i]}, device_id_type=pl.DeviceIdType.MESH,
        )

    for k in range(blocks // 2):
        a, b = 2 * k, 2 * k + 1
        tile_load(a).wait()
        tile_load(b).wait()
        acc = jnp.zeros((2 * rows, 2 * TILE_PIX), F32)
        for j in range(0, views, 2):
            lhs = jnp.concatenate(
                [
                    jnp.concatenate(
                        [filt_v[view_ref[ang_order[x] * views + j + h]] for h in range(2)], axis=1
                    )
                    for x in (a, b)
                ],
                axis=0,
            )
            rhs = jnp.concatenate(
                [
                    jnp.concatenate([tiles_v[x * views + j + h] for h in range(2)], axis=0)
                    for x in (a, b)
                ],
                axis=1,
            )
            acc = acc + jnp.dot(lhs, rhs, preferred_element_type=F32)
        send1[a] = acc[:rows, :TILE_PIX].astype(BF16)
        send1[b] = acc[rows:, TILE_PIX:].astype(BF16)
        if k == 0:
            pl.semaphore_wait(barrier, n_ang + n_gz - 2)
        send_partial(a).start()
        if b < blocks - 1:
            send_partial(b).start()

    total = acc[rows:, TILE_PIX:]
    for i in range(blocks - 1):
        peer = ang_order[i]
        pltpu.make_async_remote_copy(
            src_ref=send1.at[0], dst_ref=recv1.at[peer], send_sem=s1.at[i], recv_sem=r1.at[peer],
            device_id={"ang": peer}, device_id_type=pl.DeviceIdType.MESH,
        ).wait_recv()
        total = total + recv1[peer].astype(F32)
    high = total.astype(BF16)
    low = (total - high.astype(F32)).astype(BF16)
    placed = jnp.dot(place_v[...], jnp.concatenate([high, low], axis=0), preferred_element_type=F32)
    send2[...] = placed.astype(BF16).reshape(n_gz * n_ang, 2, TILE_PIX)

    me = gz * n_ang + ang

    def send_slices(to_gz, to_ang):
        return pltpu.make_async_remote_copy(
            src_ref=send2.at[to_gz * n_ang + to_ang], dst_ref=recv2.at[me], send_sem=s2.at[0], recv_sem=r2.at[0],
            device_id={"gz": to_gz, "ang": to_ang}, device_id_type=pl.DeviceIdType.MESH,
        )

    for at in gz_order:
        to_gz = gz_at(*at)

        def send_one(d, carry, to_gz=to_gz):
            send_slices(to_gz, lax.rem(ang + d + n_ang // 2, n_ang)).start()
            return carry

        if at == (0, 0):
            lax.fori_loop(0, n_ang // 2, send_one, 0)
            lax.fori_loop(n_ang // 2 + 1, n_ang, send_one, 0)
        else:
            lax.fori_loop(0, n_ang, send_one, 0)

    recv2[me] = send2[me]
    peers = n_gz * n_ang - 1
    everything = pltpu.make_async_remote_copy(
        src_ref=send2.at[pl.ds(0, peers)], dst_ref=recv2.at[pl.ds(0, peers)], send_sem=s2.at[0], recv_sem=r2.at[0],
        device_id={"gz": gz_peer(1)}, device_id_type=pl.DeviceIdType.MESH,
    )
    everything.wait_recv()
    summed = jnp.sum(recv2[...].astype(F32).reshape(n_gz, n_ang, 2, TILE_PIX), axis=0)
    for p in range(blocks):
        out_ref[:, p * TILE_PIX : (p + 1) * TILE_PIX] = summed[p]

    for i in range(blocks - 1):
        send_partial(i).wait_send()
    everything.wait_send()


def on_device(n_gz, n_ang, fan_views, rebin_weight, slab_table, slice_offset, tiles, tile_view):
    _, rows, views, cols = fan_views.shape
    zd = 2 * n_ang
    operator = jnp.asarray(filter_operator(cols))
    dma = pltpu.SemaphoreType.DMA
    hbm = pl.BlockSpec(memory_space=pl.ANY)
    return pl.pallas_call(
        functools.partial(kernel, n_gz, n_ang),
        out_shape=jax.ShapeDtypeStruct((2, n_ang * TILE_PIX), F32),
        in_specs=[hbm] * 7,
        out_specs=pl.BlockSpec(memory_space=pltpu.VMEM),
        scratch_shapes=[
            pltpu.VMEM((rows, views, cols), BF16),
            pltpu.VMEM((cols, cols), BF16),
            pltpu.VMEM((cols, cols), BF16),
            pltpu.VMEM((n_ang * views, cols, TILE_PIX), BF16),
            pltpu.VMEM((cols // 128 * rows * views, 128), F32),
            pltpu.VMEM((views, rows, cols), BF16),
            pltpu.VMEM((n_gz * zd, 2 * rows), BF16),
            pltpu.VMEM((n_ang, rows, TILE_PIX), BF16),
            pltpu.VMEM((n_ang, rows, TILE_PIX), BF16),
            pltpu.VMEM((n_gz * n_ang, 2, TILE_PIX), BF16),
            pltpu.VMEM((n_gz * n_ang, 2, TILE_PIX), BF16),
            pltpu.SMEM((1, rows // BR), jnp.int32),
            pltpu.SMEM((1, rows // BR), jnp.int32),
            pltpu.SMEM((n_ang * views,), jnp.int32),
            dma((6,)),
            dma((n_ang,)),
            dma((n_ang,)), dma((n_ang,)),
            dma((1,)), dma((1,)),
        ],
        compiler_params=pltpu.CompilerParams(
            collective_id=0, has_side_effects=True, vmem_limit_bytes=60 * 1024 * 1024
        ),
        name="reconstruct",
    )(slab_table[:, :, 0], slice_offset, tile_view, fan_views, rebin_weight, operator, tiles)


def solution(mesh):
    n_gz, n_ang = mesh.shape["gz"], mesh.shape["ang"]
    in_specs = (
        P("gz", None, "ang", None),
        P(),
        P("gz", None, None),
        P("gz", None),
        P("ang", None, None),
        P("ang"),
    )
    out_specs = P(("gz", "ang"), None)
    return jax.shard_map(
        functools.partial(on_device, n_gz, n_ang),
        mesh=mesh, in_specs=in_specs, out_specs=out_specs, check_vma=False,
    )
```

time: 37.1 us -> 40.5 us (1.092)
  Pallas kernels: 35.6 us -> 39 us
    pallas_call x1, Pallas kernels: 35.6 us -> 39 us  [on_device(): pl.pallas_call(functools.partial(kernel, n_gz, n_ang), out_shape=jax.Shap...]
where the time goes in v2:
time: 40.5 us; the launch traced here: 40.3 us
  Pallas kernels  39 us (96%)
  local copies, waits for them, and re-layouts  1.32 us (3%)
    pallas_call x1, Pallas kernels, on_device(): pl.pallas_call(functools.partial(kernel, n_gz, n_ang), out_shape=jax.Shap...  39 us
    unnamed x1, local copies, waits for them, and re-layouts  1.32 us

profile of v2, /device:TPU:1, one launch (start us, length us, event | category | flops | bytes accessed | tf_op | source)
XLA Modules:
  0.0 40.3 jit_solution(9604121421684871630)
XLA Ops:
  0.0 39.0 %reconstruct.1 = f32[2,2048]{1,0:T(2,128)} custom-call(s32[1,16]{1,0:T(1,128)} %bitcast.1, s32[1,16]{1,0:T(1,128)} %offset_hbm.1, s32[128]{0:T(128)} %view_hbm.1, bf16[1,64,8,896]{3,2,1,0:T(8,128)(2,1)} %fan_hbm.1, bf16[896,896]{1,0:T(8,128)(2,1)} %rebin_hbm.1, bf16[896,896]{1,0:T(8,128)(2,1)} %constant.2.clone.filter_hbm, bf16[128,896,128]{2,1,0:T(8,128)(2,1)} %tiles_hbm.1), custom_call_target="tpu_custom_call" | custom-call | tf_op jit(solution)/shard_map/reconstruct/pallas_call | solution.py:217
  39.0 1.3 %copy.9 = f32[2,2048]{1,0:T(2,128)} copy(f32[2,2048]{1,0:T(2,128)} %reconstruct.1) | data formatting | bytes 32768

commit v3 on v2

--- a/solution.py
+++ b/solution.py
@@ -30,8 +30,8 @@
     slab_hbm, offset_hbm, view_hbm, fan_hbm, rebin_hbm, filter_hbm, tiles_hbm,
     out_ref,
     fan_v, rebin_v, filter_v, tiles_v, par_v, filt_v, place_v,
-    send1, recv1, send2, recv2, slab_ref, offset_ref, view_ref,
-    in_sem, tile_sem, s1, r1, s2, r2,
+    send0, recv0, kept, send1, recv1, send2, recv2, send3, recv3, slab_ref, offset_ref, view_ref,
+    in_sem, tile_sem, s0, r0, s1, r1, s2, r2, s3, r3,
 ):
     gz, ang = lax.axis_index("gz"), lax.axis_index("ang")
     blocks, views, rows, cols = n_ang, fan_v.shape[1], fan_v.shape[0], fan_v.shape[2]
@@ -47,22 +47,15 @@
         y, z = gz // length, lax.rem(gz, length)
         return lax.rem(y + dy, 2) * length + lax.rem(z + dz, length)
 
-    ang_order = [
-        ang_at(dx, dy, dc)
-        for dx, dy in ((2, 1), (1, 1), (3, 1), (2, 0), (0, 1), (1, 0), (3, 0), (0, 0))
-        for dc in (1, 0)
-    ]
+    chips = [(2, 1), (1, 1), (3, 1), (0, 1), (2, 0), (1, 0), (3, 0), (0, 0)]
+    ang_order = [ang_at(dx, dy, dc) for dx, dy in chips for dc in (1, 0)]
     length = n_gz // 2
     gz_order = sorted(
         [(dy, dz) for dy in range(2) for dz in range(length)],
         key=lambda at: -at[0] - min(at[1], length - at[1]),
     )
 
-    def ang_peer(d):
-        return lax.rem(ang + d, n_ang)
-
-    def gz_peer(d):
-        return lax.rem(gz + d, n_gz)
+    gz_order = [gz_at(*at) for at in gz_order]
 
     loads = [
         pltpu.make_async_copy(fan_hbm.at[0], fan_v, in_sem.at[0]),
@@ -86,10 +79,10 @@
         tile_load(i).start()
 
     barrier = pltpu.get_barrier_semaphore()
-    for d in range(1, n_ang):
-        pl.semaphore_signal(barrier, inc=1, device_id={"ang": ang_peer(d)}, device_id_type=pl.DeviceIdType.MESH)
-    for d in range(1, n_gz):
-        pl.semaphore_signal(barrier, inc=1, device_id={"gz": gz_peer(d)}, device_id_type=pl.DeviceIdType.MESH)
+    for peer in gz_order[:-1]:
+        pl.semaphore_signal(barrier, inc=1, device_id={"gz": peer}, device_id_type=pl.DeviceIdType.MESH)
+    for peer in ang_order[:-1]:
+        pl.semaphore_signal(barrier, inc=1, device_id={"ang": peer}, device_id_type=pl.DeviceIdType.MESH)
 
     for load in loads[3:]:
         load.wait()
@@ -121,12 +114,23 @@
     filtered = jnp.dot(by_view, filter_v[...], preferred_element_type=F32).astype(BF16)
     filt_v[...] = filtered.reshape(views, rows, cols)
 
-    def send_partial(i):
-        return pltpu.make_async_remote_copy(
-            src_ref=send1.at[i], dst_ref=recv1.at[ang], send_sem=s1.at[i], recv_sem=r1.at[ang],
-            device_id={"ang": ang_order[i]}, device_id_type=pl.DeviceIdType.MESH,
-        )
-
+    def send_sibling(k):
+        return pltpu.make_async_remote_copy(
+            src_ref=send0.at[k], dst_ref=recv0.at[k], send_sem=s0.at[k], recv_sem=r0.at[k],
+            device_id={"ang": ang_at(0, 0, 1)}, device_id_type=pl.DeviceIdType.MESH,
+        )
+
+    def send_partial(k):
+        return pltpu.make_async_remote_copy(
+            src_ref=send1.at[k], dst_ref=recv1.at[ang // 2], send_sem=s1.at[k], recv_sem=r1.at[ang // 2],
+            device_id={"ang": ang_order[2 * k + 1]}, device_id_type=pl.DeviceIdType.MESH,
+        )
+
+    def chip_sum(k):
+        send_sibling(k).wait_recv()
+        return kept[k] + recv0[k]
+
+    last = blocks // 2 - 1
     for k in range(blocks // 2):
         a, b = 2 * k, 2 * k + 1
         tile_load(a).wait()
@@ -150,62 +154,67 @@
                 axis=1,
             )
             acc = acc + jnp.dot(lhs, rhs, preferred_element_type=F32)
-        send1[a] = acc[:rows, :TILE_PIX].astype(BF16)
-        send1[b] = acc[rows:, TILE_PIX:].astype(BF16)
+        send0[k] = acc[:rows, :TILE_PIX]
+        kept[k] = acc[rows:, TILE_PIX:]
         if k == 0:
             pl.semaphore_wait(barrier, n_ang + n_gz - 2)
-        send_partial(a).start()
-        if b < blocks - 1:
-            send_partial(b).start()
-
-    total = acc[rows:, TILE_PIX:]
-    for i in range(blocks - 1):
-        peer = ang_order[i]
+        send_sibling(k).start()
+        if k > 0:
+            send1[k - 1] = chip_sum(k - 1).astype(BF16)
+            send_partial(k - 1).start()
+
+    def wait_recv(buffer, sem, index):
         pltpu.make_async_remote_copy(
-            src_ref=send1.at[0], dst_ref=recv1.at[peer], send_sem=s1.at[i], recv_sem=r1.at[peer],
-            device_id={"ang": peer}, device_id_type=pl.DeviceIdType.MESH,
+            src_ref=buffer.at[index], dst_ref=buffer.at[index], send_sem=sem.at[index], recv_sem=sem.at[index],
+            device_id={"ang": ang_at(0, 0, 1)}, device_id_type=pl.DeviceIdType.MESH,
         ).wait_recv()
-        total = total + recv1[peer].astype(F32)
+
+    total = chip_sum(last)
+    for k in range(last):
+        chip = ang_order[2 * k + 1] // 2
+        wait_recv(recv1, r1, chip)
+        total = total + recv1[chip].astype(F32)
     high = total.astype(BF16)
     low = (total - high.astype(F32)).astype(BF16)
     placed = jnp.dot(place_v[...], jnp.concatenate([high, low], axis=0), preferred_element_type=F32)
-    send2[...] = placed.astype(BF16).reshape(n_gz * n_ang, 2, TILE_PIX)
-
-    me = gz * n_ang + ang
-
-    def send_slices(to_gz, to_ang):
-        return pltpu.make_async_remote_copy(
-            src_ref=send2.at[to_gz * n_ang + to_ang], dst_ref=recv2.at[me], send_sem=s2.at[0], recv_sem=r2.at[0],
-            device_id={"gz": to_gz, "ang": to_ang}, device_id_type=pl.DeviceIdType.MESH,
-        )
-
-    for at in gz_order:
-        to_gz = gz_at(*at)
-
-        def send_one(d, carry, to_gz=to_gz):
-            send_slices(to_gz, lax.rem(ang + d + n_ang // 2, n_ang)).start()
-            return carry
-
-        if at == (0, 0):
-            lax.fori_loop(0, n_ang // 2, send_one, 0)
-            lax.fori_loop(n_ang // 2 + 1, n_ang, send_one, 0)
-        else:
-            lax.fori_loop(0, n_ang, send_one, 0)
-
-    recv2[me] = send2[me]
-    peers = n_gz * n_ang - 1
-    everything = pltpu.make_async_remote_copy(
-        src_ref=send2.at[pl.ds(0, peers)], dst_ref=recv2.at[pl.ds(0, peers)], send_sem=s2.at[0], recv_sem=r2.at[0],
-        device_id={"gz": gz_peer(1)}, device_id_type=pl.DeviceIdType.MESH,
-    )
-    everything.wait_recv()
-    summed = jnp.sum(recv2[...].astype(F32).reshape(n_gz, n_ang, 2, TILE_PIX), axis=0)
+    send2[...] = placed.astype(BF16).reshape(n_gz, zd, TILE_PIX)
+
+    def send_slab(to):
+        return pltpu.make_async_remote_copy(
+            src_ref=send2.at[to], dst_ref=recv2.at[gz], send_sem=s2.at[to], recv_sem=r2.at[gz],
+            device_id={"gz": to}, device_id_type=pl.DeviceIdType.MESH,
+        )
+
+    for to in gz_order[:-1]:
+        send_slab(to).start()
+    slab = send2[gz].astype(F32)
+    for peer in reversed(gz_order[:-1]):
+        wait_recv(recv2, r2, peer)
+        slab = slab + recv2[peer].astype(F32)
+
+    send3[...] = slab.reshape(n_ang, 2, TILE_PIX)
+
+    def send_slices(to):
+        return pltpu.make_async_remote_copy(
+            src_ref=send3.at[to], dst_ref=recv3.at[ang], send_sem=s3.at[to], recv_sem=r3.at[ang],
+            device_id={"ang": to}, device_id_type=pl.DeviceIdType.MESH,
+        )
+
+    for to in ang_order[:-1]:
+        send_slices(to).start()
+    recv3[ang] = send3[ang]
+    for k in range(last + 1):
+        send_sibling(k).wait_send()
+    for k in range(last):
+        send_partial(k).wait_send()
+    for to in gz_order[:-1]:
+        send_slab(to).wait_send()
+    for peer in reversed(ang_order[:-1]):
+        wait_recv(recv3, r3, peer)
     for p in range(blocks):
-        out_ref[:, p * TILE_PIX : (p + 1) * TILE_PIX] = summed[p]
-
-    for i in range(blocks - 1):
-        send_partial(i).wait_send()
-    everything.wait_send()
+        out_ref[:, p * TILE_PIX : (p + 1) * TILE_PIX] = recv3[p]
+    for to in ang_order[:-1]:
+        send_slices(to).wait_send()
 
 
 def on_device(n_gz, n_ang, fan_views, rebin_weight, slab_table, slice_offset, tiles, tile_view):
@@ -227,17 +236,24 @@
             pltpu.VMEM((cols // 128 * rows * views, 128), F32),
             pltpu.VMEM((views, rows, cols), BF16),
             pltpu.VMEM((n_gz * zd, 2 * rows), BF16),
-            pltpu.VMEM((n_ang, rows, TILE_PIX), BF16),
-            pltpu.VMEM((n_ang, rows, TILE_PIX), BF16),
-            pltpu.VMEM((n_gz * n_ang, 2, TILE_PIX), BF16),
-            pltpu.VMEM((n_gz * n_ang, 2, TILE_PIX), BF16),
+            pltpu.VMEM((n_ang // 2, rows, TILE_PIX), F32),
+            pltpu.VMEM((n_ang // 2, rows, TILE_PIX), F32),
+            pltpu.VMEM((n_ang // 2, rows, TILE_PIX), F32),
+            pltpu.VMEM((n_ang // 2, rows, TILE_PIX), BF16),
+            pltpu.VMEM((n_ang // 2, rows, TILE_PIX), BF16),
+            pltpu.VMEM((n_gz, zd, TILE_PIX), BF16),
+            pltpu.VMEM((n_gz, zd, TILE_PIX), BF16),
+            pltpu.VMEM((n_ang, 2, TILE_PIX), F32),
+            pltpu.VMEM((n_ang, 2, TILE_PIX), F32),
             pltpu.SMEM((1, rows // BR), jnp.int32),
             pltpu.SMEM((1, rows // BR), jnp.int32),
             pltpu.SMEM((n_ang * views,), jnp.int32),
             dma((6,)),
             dma((n_ang,)),
+            dma((n_ang // 2,)), dma((n_ang // 2,)),
+            dma((n_ang // 2,)), dma((n_ang // 2,)),
+            dma((n_gz,)), dma((n_gz,)),
             dma((n_ang,)), dma((n_ang,)),
-            dma((1,)), dma((1,)),
         ],
         compiler_params=pltpu.CompilerParams(
             collective_id=0, has_side_effects=True, vmem_limit_bytes=60 * 1024 * 1024

time: 40.5 us -> 42.8 us (1.057)
  Pallas kernels: 39 us -> 41.3 us
    pallas_call x1, Pallas kernels: 39 us -> 41.3 us  [on_device(): pl.pallas_call(functools.partial(kernel, n_gz, n_ang), out_shape=jax.Shap...]
where the time goes in v3:
time: 42.8 us; the launch traced here: 42.6 us
  Pallas kernels  41.3 us (96%)
  local copies, waits for them, and re-layouts  1.32 us (3%)
    pallas_call x1, Pallas kernels, on_device(): pl.pallas_call(functools.partial(kernel, n_gz, n_ang), out_shape=jax.Shap...  41.3 us
    unnamed x1, local copies, waits for them, and re-layouts  1.32 us

profile of v3, /device:TPU:1, one launch (start us, length us, event | category | flops | bytes accessed | tf_op | source)
XLA Modules:
  0.0 42.6 jit_solution(14126860317765565850)
XLA Ops:
  0.0 41.3 %reconstruct.1 = f32[2,2048]{1,0:T(2,128)} custom-call(s32[1,16]{1,0:T(1,128)} %bitcast.1, s32[1,16]{1,0:T(1,128)} %offset_hbm.1, s32[128]{0:T(128)} %view_hbm.1, bf16[1,64,8,896]{3,2,1,0:T(8,128)(2,1)} %fan_hbm.1, bf16[896,896]{1,0:T(8,128)(2,1)} %rebin_hbm.1, bf16[896,896]{1,0:T(8,128)(2,1)} %constant.2.clone.filter_hbm, bf16[128,896,128]{2,1,0:T(8,128)(2,1)} %tiles_hbm.1), custom_call_target="tpu_custom_call" | custom-call | tf_op jit(solution)/shard_map/reconstruct/pallas_call | solution.py:226
  41.3 1.3 %copy.9 = f32[2,2048]{1,0:T(2,128)} copy(f32[2,2048]{1,0:T(2,128)} %reconstruct.1) | data formatting | bytes 32768

commit v4 on v3

--- a/solution.py
+++ b/solution.py
@@ -42,13 +42,16 @@
         x, y, c = ang // 4, lax.rem(ang // 2, 2), lax.rem(ang, 2)
         return lax.rem(x + dx, 4) * 4 + lax.rem(y + dy, 2) * 2 + lax.rem(c + dc, 2)
 
+    def owner(i):
+        k = i // 2
+        return ang_at(lax.rem(k + 1, 4), 1 - k // 4, 1 - lax.rem(i, 2))
+
     def gz_at(dy, dz):
         length = n_gz // 2
         y, z = gz // length, lax.rem(gz, length)
         return lax.rem(y + dy, 2) * length + lax.rem(z + dz, length)
 
-    chips = [(2, 1), (1, 1), (3, 1), (0, 1), (2, 0), (1, 0), (3, 0), (0, 0)]
-    ang_order = [ang_at(dx, dy, dc) for dx, dy in chips for dc in (1, 0)]
+    ang_order = [owner(jnp.int32(i)) for i in range(n_ang)]
     length = n_gz // 2
     gz_order = sorted(
         [(dy, dz) for dy in range(2) for dz in range(length)],
@@ -70,13 +73,16 @@
 
     def tile_load(i):
         return pltpu.make_async_copy(
-            tiles_hbm.at[pl.ds(ang_order[i] * views, views)],
+            tiles_hbm.at[pl.ds(owner(i) * views, views)],
             tiles_v.at[pl.ds(i * views, views)],
             tile_sem.at[i],
         )
 
-    for i in range(blocks):
+    def start_tile(i, carry):
         tile_load(i).start()
+        return carry
+
+    lax.fori_loop(0, blocks, start_tile, 0)
 
     barrier = pltpu.get_barrier_semaphore()
     for peer in gz_order[:-1]:
@@ -97,22 +103,38 @@
 
     loads[0].wait()
     loads[1].wait()
-    par = jnp.dot(fan_v[...].reshape(rows * views, cols), rebin_v[...], preferred_element_type=F32)
-    for c in range(cols // 128):
-        par_v[c * rows * views : (c + 1) * rows * views] = par[:, c * 128 : (c + 1) * 128]
+    step = 16
+
+    def rebin(r, carry):
+        part = fan_v[pl.ds(r * step, step)].reshape(step * views, cols)
+        par = jnp.dot(part, rebin_v[...], preferred_element_type=F32)
+        for c in range(cols // 128):
+            start = c * rows * views + r * (step * views)
+            par_v[pl.ds(pl.multiple_of(start, 8), step * views)] = par[:, c * 128 : (c + 1) * 128]
+        return carry
+
+    lax.fori_loop(0, rows // step, rebin, 0)
     loads[2].wait()
-    by_view = jnp.concatenate(
-        [
-            jnp.concatenate(
-                [par_v[pl.ds(c * rows * views + v, rows, stride=views)].astype(BF16) for c in range(cols // 128)],
-                axis=1,
-            )
-            for v in range(views)
-        ],
-        axis=0,
-    )
-    filtered = jnp.dot(by_view, filter_v[...], preferred_element_type=F32).astype(BF16)
-    filt_v[...] = filtered.reshape(views, rows, cols)
+
+    def ramp(w, carry):
+        by_view = jnp.concatenate(
+            [
+                jnp.concatenate(
+                    [
+                        par_v[pl.ds(c * rows * views + 2 * w + h, rows, stride=views)].astype(BF16)
+                        for c in range(cols // 128)
+                    ],
+                    axis=1,
+                )
+                for h in range(2)
+            ],
+            axis=0,
+        )
+        filtered = jnp.dot(by_view, filter_v[...], preferred_element_type=F32).astype(BF16)
+        filt_v[pl.ds(2 * w, 2)] = filtered.reshape(2, rows, cols)
+        return carry
+
+    lax.fori_loop(0, views // 2, ramp, 0)
 
     def send_sibling(k):
         return pltpu.make_async_remote_copy(
@@ -123,7 +145,7 @@
     def send_partial(k):
         return pltpu.make_async_remote_copy(
             src_ref=send1.at[k], dst_ref=recv1.at[ang // 2], send_sem=s1.at[k], recv_sem=r1.at[ang // 2],
-            device_id={"ang": ang_order[2 * k + 1]}, device_id_type=pl.DeviceIdType.MESH,
+            device_id={"ang": owner(2 * k + 1)}, device_id_type=pl.DeviceIdType.MESH,
         )
 
     def chip_sum(k):
@@ -131,7 +153,9 @@
         return kept[k] + recv0[k]
 
     last = blocks // 2 - 1
-    for k in range(blocks // 2):
+    pl.semaphore_wait(barrier, n_ang + n_gz - 2)
+
+    def pair(k, carry):
         a, b = 2 * k, 2 * k + 1
         tile_load(a).wait()
         tile_load(b).wait()
@@ -139,9 +163,7 @@
         for j in range(0, views, 2):
             lhs = jnp.concatenate(
                 [
-                    jnp.concatenate(
-                        [filt_v[view_ref[ang_order[x] * views + j + h]] for h in range(2)], axis=1
-                    )
+                    jnp.concatenate([filt_v[view_ref[owner(x) * views + j + h]] for h in range(2)], axis=1)
                     for x in (a, b)
                 ],
                 axis=0,
@@ -156,12 +178,16 @@
             acc = acc + jnp.dot(lhs, rhs, preferred_element_type=F32)
         send0[k] = acc[:rows, :TILE_PIX]
         kept[k] = acc[rows:, TILE_PIX:]
-        if k == 0:
-            pl.semaphore_wait(barrier, n_ang + n_gz - 2)
         send_sibling(k).start()
-        if k > 0:
+
+        @pl.when(k > 0)
+        def _():
             send1[k - 1] = chip_sum(k - 1).astype(BF16)
             send_partial(k - 1).start()
+
+        return carry
+
+    lax.fori_loop(0, blocks // 2, pair, 0)
 
     def wait_recv(buffer, sem, index):
         pltpu.make_async_remote_copy(

time: 42.8 us -> 35.7 us (0.83)
  Pallas kernels: 41.3 us -> 34.2 us
    pallas_call x1, Pallas kernels: 41.3 us -> 34.2 us  [on_device(): pl.pallas_call(functools.partial(kernel, n_gz, n_ang), out_shape=jax.Shap...]
where the time goes in v4:
time: 35.7 us; the launch traced here: 35.5 us
  Pallas kernels  34.2 us (96%)
  local copies, waits for them, and re-layouts  1.32 us (4%)
    pallas_call x1, Pallas kernels, on_device(): pl.pallas_call(functools.partial(kernel, n_gz, n_ang), out_shape=jax.Shap...  34.2 us
    unnamed x1, local copies, waits for them, and re-layouts  1.32 us

profile of v4, /device:TPU:1, one launch (start us, length us, event | category | flops | bytes accessed | tf_op | source)
XLA Modules:
  0.0 35.5 jit_solution(988662403328665642)
XLA Ops:
  0.0 34.2 %reconstruct.1 = f32[2,2048]{1,0:T(2,128)} custom-call(s32[1,16]{1,0:T(1,128)} %bitcast.1, s32[1,16]{1,0:T(1,128)} %offset_hbm.1, s32[128]{0:T(128)} %view_hbm.1, bf16[1,64,8,896]{3,2,1,0:T(8,128)(2,1)} %fan_hbm.1, bf16[896,896]{1,0:T(8,128)(2,1)} %rebin_hbm.1, bf16[896,896]{1,0:T(8,128)(2,1)} %constant.2.clone.filter_hbm, bf16[128,896,128]{2,1,0:T(8,128)(2,1)} %tiles_hbm.1), custom_call_target="tpu_custom_call" | custom-call | tf_op jit(solution)/shard_map/reconstruct/pallas_call | solution.py:252
  34.2 1.3 %copy.9 = f32[2,2048]{1,0:T(2,128)} copy(f32[2,2048]{1,0:T(2,128)} %reconstruct.1) | data formatting | bytes 32768

commit v5 on v4

--- a/solution.py
+++ b/solution.py
@@ -30,8 +30,8 @@
     slab_hbm, offset_hbm, view_hbm, fan_hbm, rebin_hbm, filter_hbm, tiles_hbm,
     out_ref,
     fan_v, rebin_v, filter_v, tiles_v, par_v, filt_v, place_v,
-    send0, recv0, kept, send1, recv1, send2, recv2, send3, recv3, slab_ref, offset_ref, view_ref,
-    in_sem, tile_sem, s0, r0, s1, r1, s2, r2, s3, r3,
+    send0, recv0, kept, direct, arrived, send1, recv1, send2, recv2, send3, recv3, slab_ref, offset_ref, view_ref,
+    in_sem, tile_sem, s0, r0, sd, rd, s1, r1, s2, r2, s3, r3,
 ):
     gz, ang = lax.axis_index("gz"), lax.axis_index("ang")
     blocks, views, rows, cols = n_ang, fan_v.shape[1], fan_v.shape[0], fan_v.shape[2]
@@ -59,6 +59,12 @@
     )
 
     gz_order = [gz_at(*at) for at in gz_order]
+
+    barrier = pltpu.get_barrier_semaphore()
+    for peer in gz_order[:-1]:
+        pl.semaphore_signal(barrier, inc=1, device_id={"gz": peer}, device_id_type=pl.DeviceIdType.MESH)
+    for peer in ang_order[:-1]:
+        pl.semaphore_signal(barrier, inc=1, device_id={"ang": peer}, device_id_type=pl.DeviceIdType.MESH)
 
     loads = [
         pltpu.make_async_copy(fan_hbm.at[0], fan_v, in_sem.at[0]),
@@ -83,12 +89,6 @@
         return carry
 
     lax.fori_loop(0, blocks, start_tile, 0)
-
-    barrier = pltpu.get_barrier_semaphore()
-    for peer in gz_order[:-1]:
-        pl.semaphore_signal(barrier, inc=1, device_id={"gz": peer}, device_id_type=pl.DeviceIdType.MESH)
-    for peer in ang_order[:-1]:
-        pl.semaphore_signal(barrier, inc=1, device_id={"ang": peer}, device_id_type=pl.DeviceIdType.MESH)
 
     for load in loads[3:]:
         load.wait()
@@ -136,6 +136,8 @@
 
     lax.fori_loop(0, views // 2, ramp, 0)
 
+    last = blocks // 2 - 1
+
     def send_sibling(k):
         return pltpu.make_async_remote_copy(
             src_ref=send0.at[k], dst_ref=recv0.at[k], send_sem=s0.at[k], recv_sem=r0.at[k],
@@ -146,13 +148,19 @@
         return pltpu.make_async_remote_copy(
             src_ref=send1.at[k], dst_ref=recv1.at[ang // 2], send_sem=s1.at[k], recv_sem=r1.at[ang // 2],
             device_id={"ang": owner(2 * k + 1)}, device_id_type=pl.DeviceIdType.MESH,
+        )
+
+    def send_direct(h):
+        core = lax.rem(ang, 2)
+        return pltpu.make_async_remote_copy(
+            src_ref=direct.at[h], dst_ref=arrived.at[core], send_sem=sd.at[h], recv_sem=rd.at[core],
+            device_id={"ang": owner(2 * (last - 1) + h)}, device_id_type=pl.DeviceIdType.MESH,
         )
 
     def chip_sum(k):
         send_sibling(k).wait_recv()
         return kept[k] + recv0[k]
 
-    last = blocks // 2 - 1
     pl.semaphore_wait(barrier, n_ang + n_gz - 2)
 
     def pair(k, carry):
@@ -178,9 +186,19 @@
             acc = acc + jnp.dot(lhs, rhs, preferred_element_type=F32)
         send0[k] = acc[:rows, :TILE_PIX]
         kept[k] = acc[rows:, TILE_PIX:]
-        send_sibling(k).start()
-
-        @pl.when(k > 0)
+
+        @pl.when(k != last - 1)
+        def _():
+            send_sibling(k).start()
+
+        @pl.when(k == last - 1)
+        def _():
+            direct[0] = send0[k].astype(BF16)
+            direct[1] = kept[k].astype(BF16)
+            for h in range(2):
+                send_direct(h).start()
+
+        @pl.when((k > 0) & (k < last))
         def _():
             send1[k - 1] = chip_sum(k - 1).astype(BF16)
             send_partial(k - 1).start()
@@ -196,8 +214,11 @@
         ).wait_recv()
 
     total = chip_sum(last)
-    for k in range(last):
-        chip = ang_order[2 * k + 1] // 2
+    for h in range(2):
+        wait_recv(arrived, rd, h)
+        total = total + arrived[h].astype(F32)
+    for k in range(last - 1):
+        chip = ang_at((3 - k) % 4, 1 - k // 4, 0) // 2
         wait_recv(recv1, r1, chip)
         total = total + recv1[chip].astype(F32)
     high = total.astype(BF16)
@@ -213,12 +234,13 @@
 
     for to in gz_order[:-1]:
         send_slab(to).start()
-    slab = send2[gz].astype(F32)
-    for peer in reversed(gz_order[:-1]):
+    halves = [send2[gz].astype(F32), jnp.zeros((zd, TILE_PIX), F32)]
+    for x, peer in enumerate(reversed(gz_order[:-1])):
         wait_recv(recv2, r2, peer)
-        slab = slab + recv2[peer].astype(F32)
-
-    send3[...] = slab.reshape(n_ang, 2, TILE_PIX)
+        halves[x % 2] = halves[x % 2] + recv2[peer].astype(F32)
+
+    for h in range(2):
+        send3[:, h] = halves[h].reshape(n_ang, 2, TILE_PIX)
 
     def send_slices(to):
         return pltpu.make_async_remote_copy(
@@ -229,16 +251,19 @@
     for to in ang_order[:-1]:
         send_slices(to).start()
     recv3[ang] = send3[ang]
+    for h in range(2):
+        send_direct(h).wait_send()
     for k in range(last + 1):
-        send_sibling(k).wait_send()
-    for k in range(last):
+        if k != last - 1:
+            send_sibling(k).wait_send()
+    for k in range(last - 1):
         send_partial(k).wait_send()
     for to in gz_order[:-1]:
         send_slab(to).wait_send()
     for peer in reversed(ang_order[:-1]):
         wait_recv(recv3, r3, peer)
-    for p in range(blocks):
-        out_ref[:, p * TILE_PIX : (p + 1) * TILE_PIX] = recv3[p]
+    for h in range(2):
+        out_ref[h] = recv3[:, h]
     for to in ang_order[:-1]:
         send_slices(to).wait_send()
 
@@ -249,9 +274,9 @@
     operator = jnp.asarray(filter_operator(cols))
     dma = pltpu.SemaphoreType.DMA
     hbm = pl.BlockSpec(memory_space=pl.ANY)
-    return pl.pallas_call(
+    pieces = pl.pallas_call(
         functools.partial(kernel, n_gz, n_ang),
-        out_shape=jax.ShapeDtypeStruct((2, n_ang * TILE_PIX), F32),
+        out_shape=jax.ShapeDtypeStruct((2, n_ang, 2, TILE_PIX), F32),
         in_specs=[hbm] * 7,
         out_specs=pl.BlockSpec(memory_space=pltpu.VMEM),
         scratch_shapes=[
@@ -265,18 +290,21 @@
             pltpu.VMEM((n_ang // 2, rows, TILE_PIX), F32),
             pltpu.VMEM((n_ang // 2, rows, TILE_PIX), F32),
             pltpu.VMEM((n_ang // 2, rows, TILE_PIX), F32),
+            pltpu.VMEM((2, rows, TILE_PIX), BF16),
+            pltpu.VMEM((2, rows, TILE_PIX), BF16),
             pltpu.VMEM((n_ang // 2, rows, TILE_PIX), BF16),
             pltpu.VMEM((n_ang // 2, rows, TILE_PIX), BF16),
             pltpu.VMEM((n_gz, zd, TILE_PIX), BF16),
             pltpu.VMEM((n_gz, zd, TILE_PIX), BF16),
-            pltpu.VMEM((n_ang, 2, TILE_PIX), F32),
-            pltpu.VMEM((n_ang, 2, TILE_PIX), F32),
+            pltpu.VMEM((n_ang, 2, 2, TILE_PIX), F32),
+            pltpu.VMEM((n_ang, 2, 2, TILE_PIX), F32),
             pltpu.SMEM((1, rows // BR), jnp.int32),
             pltpu.SMEM((1, rows // BR), jnp.int32),
             pltpu.SMEM((n_ang * views,), jnp.int32),
             dma((6,)),
             dma((n_ang,)),
             dma((n_ang // 2,)), dma((n_ang // 2,)),
+            dma((2,)), dma((2,)),
             dma((n_ang // 2,)), dma((n_ang // 2,)),
             dma((n_gz,)), dma((n_gz,)),
             dma((n_ang,)), dma((n_ang,)),
@@ -286,6 +314,7 @@
         ),
         name="reconstruct",
     )(slab_table[:, :, 0], slice_offset, tile_view, fan_views, rebin_weight, operator, tiles)
+    return (pieces[0] + pieces[1]).transpose(1, 0, 2).reshape(2, n_ang * TILE_PIX)
 
 
 def solution(mesh):

time: 35.7 us -> 35.8 us (level)
  other arithmetic: 0 us -> 1.35 us
  local copies, waits for them, and re-layouts: 1.32 us -> 0 us
    reshape x0 -> x1, other arithmetic: none -> 1.35 us  [on_device(): (pieces[0] + pieces[1]).transpose(1, 0, 2).reshape(2, n_ang * TILE_PIX)]
    unnamed x1 -> x0, local copies, waits for them, and re-layouts: 1.32 us -> none
where the time goes in v5:
time: 35.8 us; the launch traced here: 35.6 us
  Pallas kernels  34.3 us (96%)
  other arithmetic  1.35 us (4%)
    pallas_call x1, Pallas kernels, on_device(): pl.pallas_call(functools.partial(kernel, n_gz, n_ang), out_shape=jax.Shap...  34.3 us
    reshape x1, other arithmetic, on_device(): (pieces[0] + pieces[1]).transpose(1, 0, 2).reshape(2, n_ang * TILE_PIX)  1.35 us

profile of v5, /device:TPU:1, one launch (start us, length us, event | category | flops | bytes accessed | tf_op | source)
XLA Modules:
  0.0 35.6 jit_solution(404544769111210440)
XLA Ops:
  0.0 34.3 %reconstruct.1 = f32[2,16,2,128]{3,2,1,0:T(2,128)} custom-call(s32[1,16]{1,0:T(1,128)} %bitcast.7, s32[1,16]{1,0:T(1,128)} %offset_hbm.1, s32[128]{0:T(128)} %view_hbm.1, bf16[1,64,8,896]{3,2,1,0:T(8,128)(2,1)} %fan_hbm.1, bf16[896,896]{1,0:T(8,128)(2,1)} %rebin_hbm.1, bf16[896,896]{1,0:T(8,128)(2,1)} %constant.2.clone.filter_hbm, ...), custom_call_target="tpu_custom_call" | custom-call | tf_op jit(solution)/shard_map/reconstruct/pallas_call | solution.py:277
  34.3 1.4 %add_bitcast_fusion = f32[2,2048]{1,0:T(2,128)} fusion(f32[2,16,2,128]{3,2,1,0:T(2,128)} %reconstruct.1), kind=kLoop, calls=%fused_computation | loop fusion | flops 4096 | bytes 49152 | tf_op jit(solution)/shard_map/reshape | solution.py:317
